TPU v7x, 32 devices: a 4x2x2 block of a 4x4x8 slice. The times are simulated.
32 devices in a mesh: dp: 4 (over y, z), tp: 8 (over x, core).
Axes of the slice: x: 4, y: 2, z: 2, core: 2. Of those that a mesh axis runs over, the one named last changes fastest.
The devices are a block of a 4x4x8 slice.
Arguments:
- y_one: float32 [32, 256, 1280], P('dp', 'tp'), parts along dimension 0
- y_two: float32 [32, 256, 1280], P('dp', 'tp'), parts along dimension 0
- dy_one: float32 [32, 256, 1280], P('dp', 'tp'), parts along dimension 0
- dy_two: float32 [32, 256, 1280], P('dp', 'tp'), parts along dimension 0
- w_qkv: bfloat16 [2, 1280, 16, 3, 80], P(None, None, 'tp')
- w_out: bfloat16 [2, 16, 80, 1280], P(None, 'tp')
- w_up: bfloat16 [2, 1280, 5120], P(None, None, 'tp')
- w_down: bfloat16 [2, 5120, 1280], P(None, 'tp')
Outputs:
- output 1: float32 [32, 256, 1280], P('dp', 'tp'), parts along dimension 0
- output 2: float32 [32, 256, 1280], P('dp', 'tp'), parts along dimension 0
- output 3: float32 [32, 256, 1280], P('dp', 'tp'), parts along dimension 0
- output 4: float32 [32, 256, 1280], P('dp', 'tp'), parts along dimension 0
- output 5: float32 [8, 1280, 16, 3, 80], P('dp', None, 'tp'), parts along dimension 0
- output 6: float32 [8, 16, 80, 1280], P('dp', 'tp'), parts along dimension 0
- output 7: float32 [8, 1280, 5120], P('dp', None, 'tp'), parts along dimension 0
- output 8: float32 [8, 5120, 1280], P('dp', 'tp'), parts along dimension 0
There are 4 independent parts. A program takes and returns all parts, laid end to end along the dimension named above; an argument that names none is the same for every part.
All inputs are finite; a program needn't handle non-finite values.
Results may differ from a plain program's by a relative error of at most 0.0190658.
Values are sent between devices in bfloat16 or wider.
A program may use at most 768 MiB of HBM per device.

v0:
```python
import jax
import jax.numpy as jnp
from jax import lax
from jax.sharding import PartitionSpec as P

RMS_EPS = 1e-6


def rms_norm(tensor):
    return tensor * lax.rsqrt(jnp.mean(tensor * tensor, axis=-1, keepdims=True) + RMS_EPS)


def rms_back(tensor, grad_in):
    inv_rms = lax.rsqrt(jnp.mean(tensor * tensor, axis=-1, keepdims=True) + RMS_EPS)
    return inv_rms * grad_in - tensor * (inv_rms * inv_rms * inv_rms) * jnp.mean(grad_in * tensor, axis=-1, keepdims=True)


def gelu_tanh(tensor):
    return jax.nn.gelu(tensor, approximate=True)


def gather_positions(tensor):
    return lax.all_gather(tensor, "tp", axis=1, tiled=True)


def scatter_positions(tensor):
    return lax.psum_scatter(tensor, "tp", scatter_dimension=1, tiled=True)


def local_backward(y_one, y_two, dy_one, dy_two, w_qkv, w_out, w_up, w_down):
    n_layers = w_qkv.shape[0]
    attn_scale = w_qkv.shape[4] ** -0.5
    grads_qkv, grads_out, grads_up, grads_down = [], [], [], []
    for layer_idx in reversed(range(n_layers)):
        wq_layer = w_qkv[layer_idx]
        wo_layer = w_out[layer_idx]
        wu_layer = w_up[layer_idx]
        wd_layer = w_down[layer_idx]
        u_mlp = gather_positions(rms_norm(y_one).astype(jnp.bfloat16))
        pre_act = jnp.einsum("bsh,hf->bsf", u_mlp, wu_layer, preferred_element_type=jnp.float32)
        hidden, gelu_pull = jax.vjp(gelu_tanh, pre_act)
        hidden_b = hidden.astype(jnp.bfloat16)
        g_part = jnp.einsum("bsf,fh->bsh", hidden_b, wd_layer, preferred_element_type=jnp.float32)
        x_two = y_two - scatter_positions(g_part)
        cot_mlp = gather_positions(dy_two.astype(jnp.bfloat16))
        grads_down.append(jnp.einsum("bsf,bsh->fh", hidden_b, cot_mlp, preferred_element_type=jnp.float32))
        d_hidden = jnp.einsum("bsh,fh->bsf", cot_mlp, wd_layer, preferred_element_type=jnp.float32)
        d_pre = gelu_pull(d_hidden)[0].astype(jnp.bfloat16)
        grads_up.append(jnp.einsum("bsh,bsf->hf", u_mlp, d_pre, preferred_element_type=jnp.float32))
        du_mlp = jnp.einsum("bsf,hf->bsh", d_pre, wu_layer, preferred_element_type=jnp.float32)
        dy_one = dy_one + rms_back(y_one, scatter_positions(du_mlp))
        u_att = gather_positions(rms_norm(x_two).astype(jnp.bfloat16))
        qkv_all = jnp.einsum("bsh,hnjd->jbnsd", u_att, wq_layer, preferred_element_type=jnp.float32).astype(jnp.bfloat16)
        q_heads, k_heads, v_heads = qkv_all[0], qkv_all[1], qkv_all[2]
        scores = jnp.einsum("bnqd,bnkd->bnqk", q_heads, k_heads, preferred_element_type=jnp.float32) * attn_scale
        attn_prob = jax.nn.softmax(scores, axis=-1)
        prob_b = attn_prob.astype(jnp.bfloat16)
        context = jnp.einsum("bnqk,bnkd->bnqd", prob_b, v_heads, preferred_element_type=jnp.float32).astype(jnp.bfloat16)
        f_part = jnp.einsum("bnqd,ndh->bqh", context, wo_layer, preferred_element_type=jnp.float32)
        x_one = y_one - scatter_positions(f_part)
        cot_att = gather_positions(dy_one.astype(jnp.bfloat16))
        grads_out.append(jnp.einsum("bnqd,bqh->ndh", context, cot_att, preferred_element_type=jnp.float32))
        d_context = jnp.einsum("bqh,ndh->bnqd", cot_att, wo_layer, preferred_element_type=jnp.float32).astype(jnp.bfloat16)
        d_prob = jnp.einsum("bnqd,bnkd->bnqk", d_context, v_heads, preferred_element_type=jnp.float32)
        d_value = jnp.einsum("bnqk,bnqd->bnkd", prob_b, d_context, preferred_element_type=jnp.float32)
        d_scores = (attn_prob * (d_prob - jnp.sum(d_prob * attn_prob, axis=-1, keepdims=True)) * attn_scale).astype(jnp.bfloat16)
        d_query = jnp.einsum("bnqk,bnkd->bnqd", d_scores, k_heads, preferred_element_type=jnp.float32)
        d_key = jnp.einsum("bnqk,bnqd->bnkd", d_scores, q_heads, preferred_element_type=jnp.float32)
        d_qkv = jnp.stack([d_query.astype(jnp.bfloat16), d_key.astype(jnp.bfloat16), d_value.astype(jnp.bfloat16)])
        grads_qkv.append(jnp.einsum("bsh,jbnsd->hnjd", u_att, d_qkv, preferred_element_type=jnp.float32))
        du_att = jnp.einsum("jbnsd,hnjd->bsh", d_qkv, wq_layer, preferred_element_type=jnp.float32)
        dx_two = dy_two + rms_back(x_two, scatter_positions(du_att))
        y_one, y_two, dy_two = x_one, x_two, dx_two
    return (y_one, y_two, dy_one, dy_two, jnp.stack(grads_qkv[::-1]), jnp.stack(grads_out[::-1]), jnp.stack(grads_up[::-1]), jnp.stack(grads_down[::-1]))


def solution(mesh):
    state_spec = P("dp", "tp", None)
    in_specs = (state_spec, state_spec, state_spec, state_spec, P(None, None, "tp", None, None), P(None, "tp", None, None), P(None, None, "tp"), P(None, "tp", None))
    out_specs = (state_spec, state_spec, state_spec, state_spec, P("dp", None, "tp", None, None), P("dp", "tp", None, None), P("dp", None, "tp"), P("dp", "tp", None))
    return jax.shard_map(local_backward, mesh=mesh, in_specs=in_specs, out_specs=out_specs, check_vma=False)
```

profile of v0, /device:TPU:81, one launch (start us, length us, event | category | flops | bytes accessed | tf_op | source)
XLA Modules:
  0.0 851.1 jit_solution(468362682303007758)
XLA Ops:
  11.2 37.7 %all-gather.9.cloned.1.call-done = bf16[8,256,1280]{2,1,0:T(8,128)(2,1)} async-done(((bf16[8,32,1280]{2,1,0:T(8,128)(2,1)}), bf16[8,256,1280]{2,1,0:T(8,128)(2,1)}) %all-gather.9.cloned.1.call-update) | async-done | bytes 5242896 | tf_op jit(solution)/shard_map/all_gather | solution.py:23
  57.9 7.7 fusion.88
  67.9 56.5 %reduce-scatter.9.cloned.1.call-done = f32[8,32,1280]{2,1,0:T(8,128)} async-done(((f32[8,256,1280]{2,1,0:T(8,128)}), f32[8,32,1280]{2,1,0:T(8,128)}) %reduce-scatter.9.cloned.1.call-update) | async-done | bytes 1310736 | tf_op jit(solution)/shard_map/reduce_scatter | solution.py:27
  128.1 32.0 %all-gather.17.cloned.1.call-done = bf16[8,256,1280]{2,1,0:T(8,128)(2,1)} async-done(((bf16[8,32,1280]{2,1,0:T(8,128)(2,1)}), bf16[8,256,1280]{2,1,0:T(8,128)(2,1)}) %all-gather.17.cloned.1.call-update) | async-done | bytes 5242896 | tf_op jit(solution)/shard_map/all_gather | solution.py:23
  160.2 9.5 %fusion.10 = bf16[8,256,640]{2,1,0:T(8,128)(2,1)S(1)} fusion(f32[8,256,640]{2,1,0:T(8,128)} %copy-done.26, bf16[8,256,1280]{2,1,0:T(8,128)(2,1)} %all-gather.17.cloned.1.call-done, bf16[2,640,1280]{2,1,0:T(8,128)(2,1)} %param.15), kind=kOutput, calls=%fused_computation.20 | convolution fusion | flops 3381657600 | bytes 14745600 | tf_op jit(solution)/shard_map/bsh,fh->bsf/dot_general | solution.py:47
  178.4 17.0 %all-gather.11.cloned.1.call-done = bf16[8,256,1280]{2,1,0:T(8,128)(2,1)} async-done(((bf16[8,32,1280]{2,1,0:T(8,128)(2,1)}), bf16[8,256,1280]{2,1,0:T(8,128)(2,1)}) %all-gather.11.cloned.1.call-update) | async-done | bytes 5242896 | tf_op jit(solution)/shard_map/all_gather | solution.py:23
  212.2 44.0 %reduce-scatter.17.cloned.1.call-done = f32[8,32,1280]{2,1,0:T(8,128)} async-done(((f32[8,256,1280]{2,1,0:T(8,128)}), f32[8,32,1280]{2,1,0:T(8,128)}) %reduce-scatter.17.cloned.1.call-update) | async-done | bytes 1310736 | tf_op jit(solution)/shard_map/reduce_scatter | solution.py:27
  257.7 59.7 %reduce-scatter.11.cloned.1.call-done = f32[8,32,1280]{2,1,0:T(8,128)} async-done(((f32[8,256,1280]{2,1,0:T(8,128)}), f32[8,32,1280]{2,1,0:T(8,128)}) %reduce-scatter.11.cloned.1.call-update) | async-done | bytes 1310736 | tf_op jit(solution)/shard_map/reduce_scatter | solution.py:27
  325.4 29.7 %all-gather.19.cloned.1.call-done = bf16[8,256,1280]{2,1,0:T(8,128)(2,1)} async-done(((bf16[8,32,1280]{2,1,0:T(8,128)(2,1)}), bf16[8,256,1280]{2,1,0:T(8,128)(2,1)}) %all-gather.19.cloned.1.call-update) | async-done | bytes 5242896 | tf_op jit(solution)/shard_map/all_gather | solution.py:23
  364.2 8.3 fusion.126
  372.5 8.3 fusion.134
  400.1 7.6 fusion.81
  407.9 43.5 %reduce-scatter.19.cloned.1.call-done = f32[8,32,1280]{2,1,0:T(8,128)} async-done(((f32[8,256,1280]{2,1,0:T(8,128)}), f32[8,32,1280]{2,1,0:T(8,128)}) %reduce-scatter.19.cloned.1.call-update) | async-done | bytes 1310736 | tf_op jit(solution)/shard_map/reduce_scatter | solution.py:27
  452.9 59.7 %reduce-scatter.13.cloned.1.call-done = f32[8,32,1280]{2,1,0:T(8,128)} async-done(((f32[8,256,1280]{2,1,0:T(8,128)}), f32[8,32,1280]{2,1,0:T(8,128)}) %reduce-scatter.13.cloned.1.call-update) | async-done | bytes 1310736 | tf_op jit(solution)/shard_map/reduce_scatter | solution.py:27
  518.2 32.4 %all-gather.21.cloned.1.call-done = bf16[8,256,1280]{2,1,0:T(8,128)(2,1)} async-done(((bf16[8,32,1280]{2,1,0:T(8,128)(2,1)}), bf16[8,256,1280]{2,1,0:T(8,128)(2,1)}) %all-gather.21.cloned.1.call-update) | async-done | bytes 5242896 | tf_op jit(solution)/shard_map/all_gather | solution.py:23
  550.6 9.7 %fusion.17 = bf16[8,256,640]{2,1,0:T(8,128)(2,1)S(1)} fusion(f32[8,256,640]{2,1,0:T(8,128)} %copy-done.27, bf16[8,256,1280]{2,1,0:T(8,128)(2,1)} %all-gather.21.cloned.1.call-done, bf16[2,640,1280]{2,1,0:T(8,128)(2,1)} %param.15), kind=kOutput, calls=%fused_computation.27 | convolution fusion | flops 3381657600 | bytes 14745600 | tf_op jit(solution)/shard_map/bsh,fh->bsf/dot_general | solution.py:47
  568.8 17.0 %all-gather.15.cloned.1.call-done = bf16[8,256,1280]{2,1,0:T(8,128)(2,1)} async-done(((bf16[8,32,1280]{2,1,0:T(8,128)(2,1)}), bf16[8,256,1280]{2,1,0:T(8,128)(2,1)}) %all-gather.15.cloned.1.call-update) | async-done | bytes 5242896 | tf_op jit(solution)/shard_map/all_gather | solution.py:23
  603.8 43.0 %reduce-scatter.21.cloned.1.call-done = f32[8,32,1280]{2,1,0:T(8,128)} async-done(((f32[8,256,1280]{2,1,0:T(8,128)}), f32[8,32,1280]{2,1,0:T(8,128)}) %reduce-scatter.21.cloned.1.call-update) | async-done | bytes 1310736 | tf_op jit(solution)/shard_map/reduce_scatter | solution.py:27
  648.3 59.7 %reduce-scatter.15.cloned.1.call-done = f32[8,32,1280]{2,1,0:T(8,128)} async-done(((f32[8,256,1280]{2,1,0:T(8,128)}), f32[8,32,1280]{2,1,0:T(8,128)}) %reduce-scatter.15.cloned.1.call-update) | async-done | bytes 1310736 | tf_op jit(solution)/shard_map/reduce_scatter | solution.py:27
  712.5 33.5 %all-gather.23.cloned.1.call-done = bf16[8,256,1280]{2,1,0:T(8,128)(2,1)} async-done(((bf16[8,32,1280]{2,1,0:T(8,128)(2,1)}), bf16[8,256,1280]{2,1,0:T(8,128)(2,1)}) %all-gather.23.cloned.1.call-update) | async-done | bytes 5242896 | tf_op jit(solution)/shard_map/all_gather | solution.py:23
  756.1 8.3 fusion.129
  764.3 8.2 fusion.137
  772.6 8.5 convolution_bitcast_fusion
  828.2 11.7 %reduce-scatter.23.cloned.1.call-done = f32[8,32,1280]{2,1,0:T(8,128)} async-done(((f32[8,256,1280]{2,1,0:T(8,128)}), f32[8,32,1280]{2,1,0:T(8,128)}) %reduce-scatter.23.cloned.1.call-update) | async-done | bytes 1310736 | tf_op jit(solution)/shard_map/reduce_scatter | solution.py:27
  (200 shorter events, 182.8 us)
Async XLA Ops:
  7.2 41.7 %all-gather.9.cloned.1.call-start = ((), (), s32[]{:S(2)}) async-start(), calls=%async_computation.8 | async-start | bytes 5898240 | tf_op jit(solution)/shard_map/all_gather | solution.py:23
  11.1 46.8 %copy-start.19 = (bf16[2,640,1280]{2,1,0:T(8,128)(2,1)S(1)}, bf16[2,640,1280]{2,1,0:T(8,128)(2,1)}, u32[]{:S(2)}) copy-start(bf16[2,640,1280]{2,1,0:T(8,128)(2,1)} %param.15) | copy-start | bytes 9830404
  11.1 113.3 %reduce-scatter.9.cloned.1.call-start = ((), (), s32[]{:S(2)}) async-start(), calls=%async_computation.9 | async-start | bytes 11796480 | tf_op jit(solution)/shard_map/reduce_scatter | solution.py:27
  65.5 58.9 %copy-start.14 = (f32[8,32,1280]{2,1,0:T(8,128)S(1)}, f32[8,32,1280]{2,1,0:T(8,128)}, u32[]{:S(2)}) copy-start(f32[8,32,1280]{2,1,0:T(8,128)} %param.9) | copy-start | bytes 3932164
  65.6 94.6 %all-gather.17.cloned.1.call-start = ((), (), s32[]{:S(2)}) async-start(), calls=%async_computation.16 | async-start | bytes 5898240 | tf_op jit(solution)/shard_map/all_gather | solution.py:23
  67.8 127.5 %all-gather.11.cloned.1.call-start = ((), (), s32[]{:S(2)}) async-start(), calls=%async_computation.10 | async-start | bytes 5898240 | tf_op jit(solution)/shard_map/all_gather | solution.py:23
  128.0 43.1 %copy-start.21 = (bf16[2,1280,640]{2,1,0:T(8,128)(2,1)S(1)}, bf16[2,1280,640]{2,1,0:T(8,128)(2,1)}, u32[]{:S(2)}) copy-start(bf16[2,1280,640]{2,1,0:T(8,128)(2,1)} %param.14) | copy-start | bytes 9830404
  128.0 128.2 %reduce-scatter.17.cloned.1.call-start = ((), (), s32[]{:S(2)}) async-start(), calls=%async_computation.17 | async-start | bytes 11796480 | tf_op jit(solution)/shard_map/reduce_scatter | solution.py:27
  178.0 17.3 %copy-start.11 = (bf16[2,1280,2,3,80]{1,4,3,2,0:T(8,128)(2,1)S(1)}, bf16[2,1280,2,3,80]{1,4,3,2,0:T(8,128)(2,1)}, u32[]{:S(2)}) copy-start(bf16[2,1280,2,3,80]{1,4,3,2,0:T(8,128)(2,1)} %param.12) | copy-start | bytes 7372804
  178.1 139.3 %reduce-scatter.11.cloned.1.call-start = ((), (), s32[]{:S(2)}) async-start(), calls=%async_computation.11 | async-start | bytes 11796480 | tf_op jit(solution)/shard_map/reduce_scatter | solution.py:27
  212.1 44.1 %copy-start = (f32[8,32,1280]{2,1,0:T(8,128)S(1)}, f32[8,32,1280]{2,1,0:T(8,128)}, u32[]{:S(2)}) copy-start(f32[8,32,1280]{2,1,0:T(8,128)} %param.8) | copy-start | bytes 3932164
  212.1 142.9 %all-gather.19.cloned.1.call-start = ((), (), s32[]{:S(2)}) async-start(), calls=%async_computation.18 | async-start | bytes 5898240 | tf_op jit(solution)/shard_map/all_gather | solution.py:23
  321.3 69.7 %all-gather.13.cloned.1.call-start = ((), (), s32[]{:S(2)}) async-start(), calls=%async_computation.12 | async-start | bytes 5898240 | tf_op jit(solution)/shard_map/all_gather | solution.py:23
  322.4 128.9 %reduce-scatter.19.cloned.1.call-start = ((), (), s32[]{:S(2)}) async-start(), calls=%async_computation.19 | async-start | bytes 11796480 | tf_op jit(solution)/shard_map/reduce_scatter | solution.py:27
  390.5 122.1 %reduce-scatter.13.cloned.1.call-start = ((), (), s32[]{:S(2)}) async-start(), calls=%async_computation.13 | async-start | bytes 11796480 | tf_op jit(solution)/shard_map/reduce_scatter | solution.py:27
  407.7 43.7 %copy-start.3 = (f32[8,32,1280]{2,1,0:T(8,128)S(1)}, f32[8,32,1280]{2,1,0:T(8,128)}, u32[]{:S(2)}) copy-start(f32[8,32,1280]{2,1,0:T(8,128)} %copy-done.2) | copy-start | bytes 3932164
  407.8 142.8 %all-gather.21.cloned.1.call-start = ((), (), s32[]{:S(2)}) async-start(), calls=%async_computation.20 | async-start | bytes 5898240 | tf_op jit(solution)/shard_map/all_gather | solution.py:23
  516.8 324.6 %copy-start.1 = (f32[8,32,1280]{2,1,0:T(8,128)}, f32[8,32,1280]{2,1,0:T(8,128)S(1)}, u32[]{:S(2)}) copy-start(f32[8,32,1280]{2,1,0:T(8,128)S(1)} %get-tuple-element.32) | copy-start | bytes 3932164
  516.9 68.9 %all-gather.15.cloned.1.call-start = ((), (), s32[]{:S(2)}) async-start(), calls=%async_computation.14 | async-start | bytes 5898240 | tf_op jit(solution)/shard_map/all_gather | solution.py:23
  518.1 128.7 %reduce-scatter.21.cloned.1.call-start = ((), (), s32[]{:S(2)}) async-start(), calls=%async_computation.21 | async-start | bytes 11796480 | tf_op jit(solution)/shard_map/reduce_scatter | solution.py:27
  568.7 139.3 %reduce-scatter.15.cloned.1.call-start = ((), (), s32[]{:S(2)}) async-start(), calls=%async_computation.15 | async-start | bytes 11796480 | tf_op jit(solution)/shard_map/reduce_scatter | solution.py:27
  603.8 142.3 %all-gather.23.cloned.1.call-start = ((), (), s32[]{:S(2)}) async-start(), calls=%async_computation.22 | async-start | bytes 5898240 | tf_op jit(solution)/shard_map/all_gather | solution.py:23
  712.3 127.6 %reduce-scatter.23.cloned.1.call-start = ((), (), s32[]{:S(2)}) async-start(), calls=%async_computation.23 | async-start | bytes 11796480 | tf_op jit(solution)/shard_map/reduce_scatter | solution.py:27
  781.1 15.3 %slice-start.6 = ((s8[5242880]{0:T(1024)(128)(4,1)}), s8[4194304]{0:T(1024)(128)(4,1)S(1)}, s32[]{:S(2)}) async-start(s8[5242880]{0:T(1024)(128)(4,1)} %bitcast.224), calls=%async_computation.30 | async-start | bytes 8388608
  (43 other events, 202.6 us)
Sparse Core Ops, SparseCore 0:
  11.2 37.5 all-gather.8
  65.7 58.6 reduce-scatter.8
  126.6 33.5 all-gather.16
  162.2 33.1 all-gather.10
  197.5 58.6 reduce-scatter.16
  258.4 59.0 reduce-scatter.10
  321.4 33.5 all-gather.18
  357.2 33.1 all-gather.12
  392.7 58.6 reduce-scatter.18
  453.5 59.0 reduce-scatter.12
  517.0 33.5 all-gather.20
  552.6 33.1 all-gather.14
  588.1 58.6 reduce-scatter.20
  649.0 59.0 reduce-scatter.14
  712.4 33.5 all-gather.22
  781.2 58.6 reduce-scatter.22
where the time goes:
time: 859 us; the launch traced here: 851 us
  waiting for transfers between devices  578 us (67%)
  matrix products  188 us (22%)
  other arithmetic  45.7 us (5%)
  local copies, waits for them, and re-layouts  22.9 us (3%)
  between operations  15.1 us (2%)
    reduce_scatter x8, waiting for transfers between devices, scatter_positions(): return lax.psum_scatter(tensor, 'tp', scatter_dimension=1, tiled=True)  378 us
    all_gather x8, waiting for transfers between devices, gather_positions(): return lax.all_gather(tensor, 'tp', axis=1, tiled=True)  199 us
    unnamed x103, local copies, waits for them, and re-layouts  20 us
    dot_general x2, matrix products, local_backward(): jnp.einsum('bsh,fh->bsf', cot_mlp, wd_layer, preferred_element_type=jnp.f...  19.2 us
  transfers between devices with their start and end apart: 16, of which 15 were waited for; matrix products, arithmetic and copies ran while one was open for 20% of the time, Pallas kernels for 0%

commit v1 on v0

v1 whole, which is shorter than its diff:
```python
import functools

import jax
import jax.numpy as jnp
from jax import lax
from jax.experimental import pallas as pl
from jax.experimental.pallas import tpu as pltpu
from jax.sharding import PartitionSpec as P

RMS_EPS = 1e-6
f32 = jnp.float32
bf16 = jnp.bfloat16

OWN, T, W, O, PC, TP, WP, OP = range(8)
XOR = (0, 6, 2, 4, 1, 7, 3, 5)
CORE, NEAR_T, NEAR_W = 1, 6, 2
AG_SEMS = 9
RS_SEMS = 10


def peer(mask):
    me = lax.axis_index("tp")
    out = me
    for bit in (1, 2, 4):
        if mask & bit:
            out = out + bit - 2 * bit * (lax.rem(out, 2 * bit) // bit)
    return {"tp": out}


def enter(masks):
    barrier = pltpu.get_barrier_semaphore()
    for mask in masks:
        pl.semaphore_signal(barrier, inc=1, device_id=peer(mask), device_id_type=pl.DeviceIdType.MESH)
    pl.semaphore_wait(barrier, len(masks))


def remote(src, dst, send, recv, index, mask):
    return pltpu.make_async_remote_copy(
        src_ref=src, dst_ref=dst, send_sem=send.at[index], recv_sem=recv.at[index],
        device_id=peer(mask), device_id_type=pl.DeviceIdType.MESH)


class Gather:
    def __init__(self, own, buf, send, recv):
        rows = own.shape[0]
        half = rows // 2

        def at(block, lo=0, size=rows):
            return buf.at[pl.ds(block * rows + lo, size)]

        self.own, self.buf, self.rows = own, buf, rows
        self.t = remote(own, at(T), send, recv, 0, NEAR_T)
        self.w = remote(own, at(W), send, recv, 1, NEAR_W)
        self.p = remote(own, at(PC), send, recv, 2, CORE)
        self.oa = remote(at(W, 0, half), at(O, 0, half), send, recv, 3, NEAR_T)
        self.ob = remote(at(T, half, half), at(O, half, half), send, recv, 4, NEAR_W)
        self.tp = remote(at(T), at(TP), send, recv, 5, CORE)
        self.wp = remote(at(W), at(WP), send, recv, 6, CORE)
        self.opa = remote(at(O, 0, half), at(OP, 0, half), send, recv, 7, CORE)
        self.opb = remote(at(O, half, half), at(OP, half, half), send, recv, 8, CORE)

    def start(self):
        self.t.start()
        self.w.start()
        self.p.start()

    def forward(self):
        self.t.wait_recv()
        self.ob.start()
        self.tp.start()
        self.w.wait_recv()
        self.oa.start()
        self.wp.start()

    def finish(self):
        self.oa.wait_recv()
        self.opa.start()
        self.ob.wait_recv()
        self.opb.start()

    def drain(self):
        for copy in (self.t, self.w, self.p, self.oa, self.ob, self.tp, self.wp, self.opa, self.opb):
            copy.wait_send()


class Scatter:
    def __init__(self, part, bufs, send, recv):
        self.part = part
        self.snd, self.kept, self.in_o, self.in_w, self.in_t = bufs
        rows = self.in_o.shape[0]
        half = rows // 2
        lo, hi = pl.ds(0, half), pl.ds(half, half)
        self.lo, self.hi = lo, hi
        self.d2d = [remote(self.snd.at[i % 2], self.kept.at[block], send, recv, i, CORE)
                    for i, block in enumerate((O, W, T, OWN))]
        self.oa = remote(self.kept.at[O, lo], self.in_o.at[lo], send, recv, 4, NEAR_T)
        self.ob = remote(self.kept.at[O, hi], self.in_o.at[hi], send, recv, 5, NEAR_W)
        self.w_hi = remote(self.kept.at[W, hi], self.in_w.at[hi], send, recv, 6, NEAR_W)
        self.t_lo = remote(self.kept.at[T, lo], self.in_t.at[lo], send, recv, 7, NEAR_T)
        self.w_lo = remote(self.kept.at[W, lo], self.in_w.at[lo], send, recv, 8, NEAR_W)
        self.t_hi = remote(self.kept.at[T, hi], self.in_t.at[hi], send, recv, 9, NEAR_T)

    def add(self, block):
        self.part(block, self.kept.at[block], True)

    def begin(self):
        for i, block in enumerate((OP, WP, TP, PC)):
            if i >= 2:
                self.d2d[i - 2].wait_send()
            self.part(block, self.snd.at[i % 2], False)
            self.d2d[i].start()
        self.d2d[0].wait_recv()
        self.add(O)
        self.oa.start()
        self.ob.start()
        self.d2d[1].wait_recv()
        self.add(W)
        self.w_hi.start()
        self.d2d[2].wait_recv()
        self.add(T)
        self.t_lo.start()
        self.d2d[3].wait_recv()
        self.add(OWN)

    def middle(self):
        self.oa.wait_recv()
        self.kept[W, self.lo] = self.kept[W, self.lo] + self.in_o[self.lo]
        self.w_lo.start()
        self.ob.wait_recv()
        self.kept[T, self.hi] = self.kept[T, self.hi] + self.in_o[self.hi]
        self.t_hi.start()

    def end(self, out):
        for copy in (self.w_hi, self.t_lo, self.w_lo, self.t_hi):
            copy.wait_recv()
        out[...] = self.kept[OWN] + self.in_w[...] + self.in_t[...]

    def drain(self):
        for copy in (self.d2d[2], self.d2d[3], self.oa, self.ob, self.w_hi, self.t_lo, self.w_lo, self.t_hi):
            copy.wait_send()


def dot(left, right, dims):
    return lax.dot_general(left, right, (dims, ((), ())), preferred_element_type=f32)


NN, NT, TN = ((1,), (0,)), ((1,), (1,)), ((0,), (0,))


def tiles(total, size, body):
    def step(i, carry):
        body(pl.ds(pl.multiple_of(i * size, size), size))
        return carry
    lax.fori_loop(0, total // size, step, 0)


def mlp_kernel(u_ref, c_ref, w1, w2, g_ref, du_ref, dw1, dw2, u_all, c_all, act, hid, dpre,
               g_snd, g_kept, g_o, g_w, g_t, d_snd, d_kept, d_o, d_w, d_t,
               us, ur, cs, cr, gs, gr, ds, dr):
    enter((CORE, NEAR_T, NEAR_W))
    rows, hidden = u_ref.shape
    cols = w1.shape[1]
    tile = 128
    gu = Gather(u_ref, u_all, us, ur)
    gc = Gather(c_ref, c_all, cs, cr)

    def block_rows(block):
        return pl.ds(block * rows, rows)

    def up(block):
        here = block_rows(block)
        src = u_ref if block == OWN else u_all.at[here]

        def body(col):
            a = dot(src[...], w1[:, col], NN)
            hid[here, col] = jax.nn.gelu(a, approximate=True).astype(bf16)
            act[here, col] = a
        tiles(cols, tile, body)

    def down(block):
        here = block_rows(block)
        src = c_ref if block == OWN else c_all.at[here]

        def body(col):
            dh = dot(src[...], w2[col, :], NT)
            _, pull = jax.vjp(lambda a: jax.nn.gelu(a, approximate=True), act[here, col])
            dpre[here, col] = pull(dh)[0].astype(bf16)
        tiles(cols, tile, body)

    def part_of(lhs, rhs, transposed):
        def part(block, out, accumulate):
            here = block_rows(block)

            def body(col):
                value = dot(lhs[here], rhs[col, :], NT) if transposed else dot(lhs[here], rhs[:, col], NN)
                out[:, col] = out[:, col] + value if accumulate else value
            tiles(hidden, 256, body)
        return part

    rs_g = Scatter(part_of(hid, w2, False), (g_snd, g_kept, g_o, g_w, g_t), gs, gr)
    rs_d = Scatter(part_of(dpre, w1, True), (d_snd, d_kept, d_o, d_w, d_t), ds, dr)

    gu.start()
    u_all[block_rows(OWN)] = u_ref[...]
    up(OWN)
    gu.p.wait_recv()
    up(PC)
    gu.forward()
    gc.start()
    c_all[block_rows(OWN)] = c_ref[...]
    up(T)
    up(W)
    gu.tp.wait_recv()
    up(TP)
    gu.wp.wait_recv()
    up(WP)
    gu.finish()
    up(O)
    gu.opa.wait_recv()
    gu.opb.wait_recv()
    up(OP)
    down(OWN)
    gc.p.wait_recv()
    down(PC)
    gc.forward()
    rs_g.begin()
    down(T)
    down(W)
    gc.tp.wait_recv()
    down(TP)
    gc.wp.wait_recv()
    down(WP)
    gc.finish()
    rs_g.middle()
    down(O)
    gc.opa.wait_recv()
    gc.opb.wait_recv()
    down(OP)
    rs_d.begin()

    def body1(col):
        dw1[:, col] = dot(u_all[...], dpre[:, col], TN)

    def body2(col):
        dw2[col, :] = dot(hid[:, col], c_all[...], TN)
    tiles(cols, tile, body2)
    rs_d.middle()
    rs_g.end(g_ref)
    tiles(cols, tile, body1)
    rs_d.end(du_ref)
    for item in (gu, gc, rs_g, rs_d):
        item.drain()


def attn_kernel(scale, u_ref, c_ref, wq, wk, wv, wo, f_ref, du_ref, dwq, dwk, dwv, dwo,
                u_all, c_all, wo_all, q_all, k_all, v_all, dctx, ctx, ctx_in, prob,
                d_snd, d_kept, d_o, d_w, d_t, us, ur, cs, cr, ws, wr, xs, xr, ds, dr):
    enter(XOR[1:])
    rows, hidden = u_ref.shape
    width = wq.shape[1]
    head = width // 2
    pos = 32
    n_seq = rows // pos
    gu = Gather(u_ref, u_all, us, ur)
    gc = Gather(c_ref, c_all, cs, cr)
    gw = Gather(wo, wo_all, ws, wr)
    lanes = lax.broadcasted_iota(jnp.int32, (1, width), 1)
    masks = [(lanes < head), (lanes >= head)]

    def block_rows(block):
        return pl.ds(block * rows, rows)

    def pick(value, n):
        return jnp.where(masks[n], value, jnp.zeros_like(value))

    def qkv(block):
        here = block_rows(block)
        src = u_ref if block == OWN else u_all.at[here]
        value = src[...]
        for weight, out in ((wq, q_all), (wk, k_all), (wv, v_all)):
            out[here] = dot(value, weight[...], NN).astype(bf16)

    def d_ctx(block):
        here = block_rows(block)
        src = c_ref if block == OWN else c_all.at[here]
        dctx[here] = dot(src[...], wo[...], NT).astype(bf16)

    def seq_get(ref, seq):
        return jnp.concatenate([ref[pl.ds(pl.multiple_of(b * rows + seq * pos, pos), pos)] for b in range(8)], axis=0)

    def seq_put(ref, seq, value):
        for b in range(8):
            ref[pl.ds(pl.multiple_of(b * rows + seq * pos, pos), pos)] = value[b * pos:(b + 1) * pos]

    def forward(seq, carry):
        q, k, v = seq_get(q_all, seq), seq_get(k_all, seq), seq_get(v_all, seq)
        total = None
        for n in range(2):
            scores = dot(pick(q, n), k, NT) * scale
            expd = jnp.exp(scores - jnp.max(scores, axis=-1, keepdims=True))
            p = expd / jnp.sum(expd, axis=-1, keepdims=True)
            prob[2 * seq + n] = p
            out = dot(p.astype(bf16), pick(v, n), NN)
            total = out if total is None else total + out
        seq_put(ctx, seq, total.astype(bf16))
        return carry

    def backward(seq, carry):
        q, k, v, do = seq_get(q_all, seq), seq_get(k_all, seq), seq_get(v_all, seq), seq_get(dctx, seq)
        sums = [None, None, None]
        for n in range(2):
            p = prob[2 * seq + n]
            dp = dot(pick(do, n), v, NT)
            terms = [None, None, dot(p.astype(bf16), pick(do, n), TN)]
            dsc = (p * (dp - jnp.sum(dp * p, axis=-1, keepdims=True)) * scale).astype(bf16)
            terms[0] = dot(dsc, pick(k, n), NN)
            terms[1] = dot(dsc, pick(q, n), TN)
            sums = [b if a is None else a + b for a, b in zip(sums, terms)]
        for ref, value in zip((q_all, k_all, v_all), sums):
            seq_put(ref, seq, value.astype(bf16))
        return carry

    def part(block, out, accumulate):
        here = block_rows(block)

        def body(col):
            value = dot(q_all[here], wq[col, :], NT) + dot(k_all[here], wk[col, :], NT) + dot(v_all[here], wv[col, :], NT)
            out[:, col] = out[:, col] + value if accumulate else value
        tiles(hidden, 256, body)

    rs_d = Scatter(part, (d_snd, d_kept, d_o, d_w, d_t), ds, dr)
    out_rows = wo.shape[0]
    shares = [remote(ctx.at[block_rows(b)], ctx_in.at[b], xs, xr, b - 1, XOR[b]) for b in range(1, 8)]

    gu.start()
    u_all[block_rows(OWN)] = u_ref[...]
    qkv(OWN)
    gu.p.wait_recv()
    qkv(PC)
    gu.forward()
    gc.start()
    c_all[block_rows(OWN)] = c_ref[...]
    wo_all[pl.ds(0, out_rows)] = wo[...]
    qkv(T)
    qkv(W)
    gu.tp.wait_recv()
    qkv(TP)
    gu.wp.wait_recv()
    qkv(WP)
    gu.finish()
    qkv(O)
    gu.opa.wait_recv()
    gu.opb.wait_recv()
    qkv(OP)
    lax.fori_loop(0, n_seq, forward, 0)
    gc.forward()
    for copy in shares:
        copy.start()
    gw.start()
    d_ctx(OWN)
    gc.p.wait_recv()
    d_ctx(PC)
    d_ctx(T)
    d_ctx(W)
    gc.tp.wait_recv()
    d_ctx(TP)
    gc.wp.wait_recv()
    d_ctx(WP)
    gc.finish()
    d_ctx(O)
    gc.opa.wait_recv()
    gc.opb.wait_recv()
    d_ctx(OP)
    lax.fori_loop(0, n_seq, backward, 0)
    rs_d.begin()
    gw.forward()
    dwo[...] = dot(ctx[...], c_all[...], TN)
    gw.finish()
    rs_d.middle()
    dwq[...] = dot(u_all[...], q_all[...], TN)
    dwk[...] = dot(u_all[...], k_all[...], TN)
    dwv[...] = dot(u_all[...], v_all[...], TN)
    for copy in shares:
        copy.wait_recv()
    for copy in (gw.p, gw.tp, gw.wp, gw.opa, gw.opb):
        copy.wait_recv()

    def f_body(col):
        total = dot(ctx[block_rows(OWN)], wo_all[pl.ds(0, out_rows), col], NN)
        for b in range(1, 8):
            total = total + dot(ctx_in[b], wo_all[pl.ds(b * out_rows, out_rows), col], NN)
        f_ref[:, col] = total
    tiles(hidden, 256, f_body)
    rs_d.end(du_ref)
    for item in (gu, gc, gw, rs_d):
        item.drain()
    for copy in shares:
        copy.wait_send()


def vmem(shape, dtype):
    return pltpu.VMEM(shape, dtype)


def scatter_scratch(rows, hidden):
    return [vmem((2, rows, hidden), f32), vmem((4, rows, hidden), f32)] + [vmem((rows, hidden), f32)] * 3


def sems(count):
    return [pltpu.SemaphoreType.DMA((count,))] * 2


def call(kernel, outs, scratch, collective_id, name, flops, *args):
    spec = pl.BlockSpec(memory_space=pltpu.VMEM)
    return pl.pallas_call(
        kernel,
        out_shape=[jax.ShapeDtypeStruct(shape, f32) for shape in outs],
        in_specs=[spec] * len(args),
        out_specs=[spec] * len(outs),
        scratch_shapes=scratch,
        name=name,
        cost_estimate=pl.CostEstimate(flops=flops, bytes_accessed=10 ** 7, transcendentals=0),
        compiler_params=pltpu.CompilerParams(
            collective_id=collective_id, has_side_effects=True, vmem_limit_bytes=67043328),
    )(*args)


def mlp_block(u, c, w1, w2):
    rows, hidden = u.shape
    cols = w1.shape[1]
    total = 8 * rows
    scratch = [vmem((total, hidden), bf16)] * 2 + [vmem((total, cols), f32)] + [vmem((total, cols), bf16)] * 2
    scratch += scatter_scratch(rows, hidden) * 2 + sems(AG_SEMS) * 2 + sems(RS_SEMS) * 2
    outs = [(rows, hidden)] * 2 + [(hidden, cols), (cols, hidden)]
    return call(mlp_kernel, outs, scratch, 0, "mlp_block", 12 * total * hidden * cols, u, c, w1, w2)


def attn_block(scale, u, c, wq, wk, wv, wo):
    rows, hidden = u.shape
    width = wq.shape[1]
    total = 8 * rows
    scratch = [vmem((total, hidden), bf16)] * 2 + [vmem((8 * wo.shape[0], hidden), bf16)]
    scratch += [vmem((total, width), bf16)] * 5 + [vmem((8, rows, width), bf16), vmem((16, 256, 256), f32)]
    scratch += scatter_scratch(rows, hidden) + sems(AG_SEMS) * 3 + sems(7) + sems(RS_SEMS)
    outs = [(rows, hidden)] * 2 + [(hidden, width)] * 3 + [(width, hidden)]
    kernel = functools.partial(attn_kernel, scale)
    return call(kernel, outs, scratch, 1, "attn_block", 24 * total * hidden * width, u, c, wq, wk, wv, wo)


def inv_rms_of(tensor):
    return lax.rsqrt(jnp.mean(tensor * tensor, axis=-1, keepdims=True) + RMS_EPS)


def rms_norm(tensor):
    return tensor * inv_rms_of(tensor)


def rms_back(tensor, grad_in):
    inv_rms = inv_rms_of(tensor)
    return inv_rms * grad_in - tensor * (inv_rms * inv_rms * inv_rms) * jnp.mean(grad_in * tensor, axis=-1, keepdims=True)


def local_backward(y_one, y_two, dy_one, dy_two, w_qkv, w_out, w_up, w_down):
    n_layers, hidden, heads, _, head_dim = w_qkv.shape
    width = heads * head_dim
    state_shape = y_one.shape
    y_one, y_two, dy_one, dy_two = [x.reshape(-1, hidden) for x in (y_one, y_two, dy_one, dy_two)]
    grads_qkv, grads_out, grads_up, grads_down = [], [], [], []
    for layer in reversed(range(n_layers)):
        wq, wk, wv = [w_qkv[layer, :, :, j].reshape(hidden, width) for j in range(3)]
        wo = w_out[layer].reshape(width, hidden)
        g_out, du_mlp, dw_up, dw_down = mlp_block(
            rms_norm(y_one).astype(bf16), dy_two.astype(bf16), w_up[layer], w_down[layer])
        x_two = y_two - g_out
        dy_one = dy_one + rms_back(y_one, du_mlp)
        f_out, du_att, dwq, dwk, dwv, dwo = attn_block(
            head_dim ** -0.5, rms_norm(x_two).astype(bf16), dy_one.astype(bf16), wq, wk, wv, wo)
        x_one = y_one - f_out
        dx_two = dy_two + rms_back(x_two, du_att)
        grads_up.append(dw_up)
        grads_down.append(dw_down)
        grads_out.append(dwo.reshape(heads, head_dim, hidden))
        grads_qkv.append(jnp.stack([g.reshape(hidden, heads, head_dim) for g in (dwq, dwk, dwv)], axis=2))
        y_one, y_two, dy_two = x_one, x_two, dx_two
    state = [x.reshape(state_shape) for x in (y_one, y_two, dy_one, dy_two)]
    return (*state, jnp.stack(grads_qkv[::-1]), jnp.stack(grads_out[::-1]), jnp.stack(grads_up[::-1]), jnp.stack(grads_down[::-1]))


def solution(mesh):
    state_spec = P("dp", "tp", None)
    in_specs = (state_spec, state_spec, state_spec, state_spec, P(None, None, "tp", None, None), P(None, "tp", None, None), P(None, None, "tp"), P(None, "tp", None))
    out_specs = (state_spec, state_spec, state_spec, state_spec, P("dp", None, "tp", None, None), P("dp", "tp", None, None), P("dp", None, "tp"), P("dp", "tp", None))
    return jax.shard_map(local_backward, mesh=mesh, in_specs=in_specs, out_specs=out_specs, check_vma=False)
```

time: 859 us -> 619 us (0.72)
  waiting for transfers between devices: 578 us -> 0 us
  Pallas kernels: 0 us -> 541 us
  matrix products: 188 us -> 0 us
  between operations: 15.1 us -> 1.19 us
  local copies, waits for them, and re-layouts: 22.9 us -> 35.6 us
    pallas_call x0 -> x4, Pallas kernels: none -> 541 us  [call(): pl.pallas_call(kernel, out_shape=[jax.ShapeDtypeStruct(shape, f32) for sh...]
    reduce_scatter x8 -> x0, waiting for transfers between devices: 378 us -> none  [scatter_positions(): return lax.psum_scatter(tensor, 'tp', scatter_dimension=1, tiled=True)]
    all_gather x8 -> x0, waiting for transfers between devices: 199 us -> none  [gather_positions(): return lax.all_gather(tensor, 'tp', axis=1, tiled=True)]
    dot_general x36 -> x0, matrix products: 188 us -> none  [the longest x2 19.2 us: local_backward(): jnp.einsum('bsh,fh->bsf', cot_mlp, wd_layer, preferred_element_type=jnp.f...]
    another operation x0 -> x6, local copies, waits for them, and re-layouts: none -> 10.6 us  [local_backward(): w_qkv[layer, :, :, j].reshape(hidden, width)]
    unnamed x103 -> x87, local copies, waits for them, and re-layouts: 20 us -> 11.1 us
    convert_element_type x8, other arithmetic: 18.5 us -> 9.71 us  [the longest x2 3.29 us: local_backward(): dy_one.astype(bf16)]
  transfers between devices with their start and end apart: 16 -> 0, of which waited for: 15 -> 0; matrix products, arithmetic and copies ran while one was open for 20% -> 0% of each run, Pallas kernels for 0% -> 0%
where the time goes in v1:
time: 619 us; the launch traced here: 616 us
  Pallas kernels  541 us (87%)
  other arithmetic  38.3 us (6%)
  local copies, waits for them, and re-layouts  35.6 us (6%)
    pallas_call x4, Pallas kernels, call(): pl.pallas_call(kernel, out_shape=[jax.ShapeDtypeStruct(shape, f32) for sh...  541 us

profile of v1, /device:TPU:81, one launch (start us, length us, event | category | flops | bytes accessed | tf_op | source)
XLA Modules:
  0.0 615.6 jit_solution(4801192675811713397)
XLA Ops:
  9.3 2.2 copy.37.wq
  11.5 2.1 copy.33.wv
  13.6 2.1 copy.32.wk
  15.7 2.1 copy.31.wq
  17.8 2.0 slice_bitcast_fusion.1
  20.9 1.9 slice_bitcast_fusion
  22.8 141.6 %mlp_block.2 = (f32[256,1280]{1,0:T(8,128)}, f32[256,1280]{1,0:T(8,128)}, f32[1280,640]{1,0:T(8,128)}, f32[640,1280]{1,0:T(8,128)}) custom-call(bf16[256,1280]{1,0:T(8,128)(2,1)} %fusion.u_ref, bf16[256,1280]{1,0:T(8,128)(2,1)} %bitcast_convert_fusion.c_ref, bf16[1280,640]{1,0:T(8,128)(2,1)} %get-tuple-element.71.w1, bf16[640,1280]{1,0:T(8,128)(2,1)} %get-tuple-element.69.w2), custom_call_target="tpu_custom_call" | custom-call | flops 20132659200 | bytes 10000000 | tf_op jit(solution)/shard_map/mlp_block/pallas_call | solution.py:415
  164.5 3.0 multiply_reduce_fusion.5
  168.1 1.6 fusion.6
  170.8 129.6 %attn_block.2 = (f32[256,1280]{1,0:T(8,128)}, f32[256,1280]{1,0:T(8,128)}, f32[1280,160]{1,0:T(8,128)}, f32[1280,160]{1,0:T(8,128)}, f32[1280,160]{1,0:T(8,128)}, /*index=5*/f32[160,1280]{1,0:T(8,128)}) custom-call(bf16[256,1280]{1,0:T(8,128)(2,1)} %multiply_convert_fusion.2.u_ref, bf16[256,1280]{1,0:T(8,128)(2,1)} %get-tuple-element.64.c_ref, ...), custom_call_target="tpu_custom_call" | custom-call | flops 10066329600 | bytes 10000000 | tf_op jit(solution)/shard_map/attn_block/pallas_call | solution.py:415
  300.3 2.1 multiply_reduce_fusion.3
  308.0 1.8 copy.43
  310.2 1.7 copy.45
  311.9 1.6 maximum_bitcast_fusion.1
  313.5 140.1 %mlp_block.3 = (f32[256,1280]{1,0:T(8,128)}, f32[256,1280]{1,0:T(8,128)}, f32[1280,640]{1,0:T(8,128)}, f32[640,1280]{1,0:T(8,128)}) custom-call(bf16[256,1280]{1,0:T(8,128)(2,1)} %multiply_convert_fusion.1.u_ref, bf16[256,1280]{1,0:T(8,128)(2,1)} %get-tuple-element.60.c_ref, bf16[1280,640]{1,0:T(8,128)(2,1)} %get-tuple-element.70.w1, ...), custom_call_target="tpu_custom_call" | custom-call | flops 20132659200 | bytes 10000000 | tf_op jit(solution)/shard_map/mlp_block/pallas_call | solution.py:415
  453.6 2.1 multiply_reduce_fusion.2
  456.3 5.7 pad_maximum_fusion
  463.4 1.6 fusion.4
  467.3 3.2 pad_maximum_fusion.1
  470.5 129.3 %attn_block.3 = (f32[256,1280]{1,0:T(8,128)}, f32[256,1280]{1,0:T(8,128)}, f32[1280,160]{1,0:T(8,128)}, f32[1280,160]{1,0:T(8,128)}, f32[1280,160]{1,0:T(8,128)}, /*index=5*/f32[160,1280]{1,0:T(8,128)}) custom-call(bf16[256,1280]{1,0:T(8,128)(2,1)} %multiply_convert_fusion.u_ref, bf16[256,1280]{1,0:T(8,128)(2,1)} %get-tuple-element.56.c_ref, ...), custom_call_target="tpu_custom_call" | custom-call | flops 10066329600 | bytes 10000000 | tf_op jit(solution)/shard_map/attn_block/pallas_call | solution.py:415
  599.8 3.1 sub.30
  605.6 1.8 copy.40
  607.8 1.7 copy.42
  611.5 2.6 copy.46
  (116 shorter events, 27.9 us)
Async XLA Ops:
  2.3 2.5 copy-start.31
  9.3 8.5 %copy-start.18 = (bf16[2,1280,640]{2,1,0:T(8,128)(2,1)S(1)}, bf16[2,1280,640]{2,1,0:T(8,128)(2,1)}, u32[]{:S(2)}) copy-start(bf16[2,1280,640]{2,1,0:T(8,128)(2,1)} %param.14) | copy-start | bytes 9830404
  17.8 3.1 copy-start.19
  164.4 3.7 copy-start.1
  164.4 3.7 copy-start.17
  164.4 3.7 copy-start.27
  164.4 3.7 copy-start.32
  164.5 3.7 copy-start.41
  300.3 2.5 copy-start.24
  302.8 2.6 copy-start.14
  302.8 2.6 copy-start.36
  302.8 2.6 copy-start.40
  303.1 4.0 copy-start.3
  303.7 3.4 copy-start.33
  453.6 2.7 copy-start.21
  455.7 9.9 %copy-start.7 = (f32[256,1280]{1,0:T(8,128)}, f32[256,1280]{1,0:T(8,128)S(1)}, u32[]{:S(2)}) copy-start(f32[256,1280]{1,0:T(8,128)S(1)} %get-tuple-element.59) | copy-start | bytes 3932164
  456.3 5.7 copy-start.4
  456.3 5.7 copy-start.11
  463.4 3.2 copy-start.20
  463.4 3.9 copy-start.22
  599.8 3.1 copy-start.8
  599.8 3.1 copy-start.12
  611.5 2.6 copy-start.29
  611.5 2.6 copy-start.30
  (19 other events, 32.0 us)

commit v2 on v0

v2 whole, which is shorter than its diff:
```python
import functools

import jax
import jax.numpy as jnp
from jax import lax
from jax.experimental import pallas as pl
from jax.experimental.pallas import tpu as pltpu
from jax.sharding import PartitionSpec as P

RMS_EPS = 1e-6
f32 = jnp.float32
bf16 = jnp.bfloat16

OWN, T, W, O, PC, TP, WP, OP = range(8)
XOR = (0, 6, 2, 4, 1, 7, 3, 5)
CORE, NEAR_T, NEAR_W = 1, 6, 2
AG_SEMS = 9
RS_SEMS = 10
NN, NT, TN = ((1,), (0,)), ((1,), (1,)), ((0,), (0,))


def peer(mask):
    out = lax.axis_index("tp")
    for bit in (1, 2, 4):
        if mask & bit:
            out = out + bit - 2 * bit * (lax.rem(out, 2 * bit) // bit)
    return {"tp": out}


def enter(masks):
    barrier = pltpu.get_barrier_semaphore()
    for mask in masks:
        pl.semaphore_signal(barrier, inc=1, device_id=peer(mask), device_id_type=pl.DeviceIdType.MESH)
    pl.semaphore_wait(barrier, len(masks))


def remote(src, dst, send, recv, index, mask):
    return pltpu.make_async_remote_copy(
        src_ref=src, dst_ref=dst, send_sem=send.at[index], recv_sem=recv.at[index],
        device_id=peer(mask), device_id_type=pl.DeviceIdType.MESH)


def dot(left, right, dims):
    return lax.dot_general(left, right, (dims, ((), ())), preferred_element_type=f32)


def loop(count, body):
    def step(i, carry):
        body(i)
        return carry
    lax.fori_loop(0, count, step, 0)


def tiles(total, size, body):
    loop(total // size, lambda i: body(pl.ds(pl.multiple_of(i * size, size), size)))


class Gather:
    def __init__(self, buf, send, recv):
        rows = buf.shape[0] // 8
        half = rows // 2

        def at(block, lo=0, size=rows):
            return buf.at[pl.ds(block * rows + lo, size)]

        self.t = remote(at(OWN), at(T), send, recv, 0, NEAR_T)
        self.w = remote(at(OWN), at(W), send, recv, 1, NEAR_W)
        self.p = remote(at(OWN), at(PC), send, recv, 2, CORE)
        self.oa = remote(at(W, 0, half), at(O, 0, half), send, recv, 3, NEAR_T)
        self.ob = remote(at(T, half, half), at(O, half, half), send, recv, 4, NEAR_W)
        self.tp = remote(at(T), at(TP), send, recv, 5, CORE)
        self.wp = remote(at(W), at(WP), send, recv, 6, CORE)
        self.opa = remote(at(O, 0, half), at(OP, 0, half), send, recv, 7, CORE)
        self.opb = remote(at(O, half, half), at(OP, half, half), send, recv, 8, CORE)

    def start(self):
        self.t.start()
        self.w.start()
        self.p.start()

    def forward(self):
        self.t.wait_recv()
        self.ob.start()
        self.tp.start()
        self.w.wait_recv()
        self.oa.start()
        self.wp.start()

    def finish(self):
        self.oa.wait_recv()
        self.opa.start()
        self.ob.wait_recv()
        self.opb.start()

    def last(self):
        self.opa.wait_recv()
        self.opb.wait_recv()

    def drain(self):
        for copy in (self.t, self.w, self.p, self.oa, self.ob, self.tp, self.wp, self.opa, self.opb):
            copy.wait_send()

    def each_block(self, compute, after_forward=None, forwarded=False):
        def body(step):
            if not forwarded:
                @pl.when(step == 2)
                def _():
                    self.forward()
                    if after_forward is not None:
                        after_forward()
            for when, act in ((1, self.p.wait_recv), (3, self.tp.wait_recv), (5, self.wp.wait_recv), (6, self.finish), (7, self.last)):
                pl.when(step == when)(act)
            compute(step // 2 + 4 * lax.rem(step, 2))
        loop(8, body)


class Scatter:
    def __init__(self, part, bufs, send, recv):
        self.part, self.send, self.recv = part, send, recv
        self.snd, self.kept, self.in_o, self.in_w, self.in_t = bufs
        half = self.in_o.shape[0] // 2
        lo, hi = pl.ds(0, half), pl.ds(half, half)
        self.lo, self.hi = lo, hi
        self.oa = remote(self.kept.at[O, lo], self.in_o.at[lo], send, recv, 4, NEAR_T)
        self.ob = remote(self.kept.at[O, hi], self.in_o.at[hi], send, recv, 5, NEAR_W)
        self.w_hi = remote(self.kept.at[W, hi], self.in_w.at[hi], send, recv, 6, NEAR_W)
        self.t_lo = remote(self.kept.at[T, lo], self.in_t.at[lo], send, recv, 7, NEAR_T)
        self.w_lo = remote(self.kept.at[W, lo], self.in_w.at[lo], send, recv, 8, NEAR_W)
        self.t_hi = remote(self.kept.at[T, hi], self.in_t.at[hi], send, recv, 9, NEAR_T)

    def d2d(self, i):
        return remote(self.snd.at[lax.rem(i, 2)], self.kept.at[3 - i], self.send, self.recv, i, CORE)

    def begin(self):
        def theirs(i):
            @pl.when(i >= 2)
            def _():
                self.d2d(i - 2).wait_send()
            self.part(7 - i, self.snd.at[lax.rem(i, 2)], False)
            self.d2d(i).start()
        loop(4, theirs)

        def mine(i):
            self.d2d(i).wait_recv()
            self.part(3 - i, self.kept.at[3 - i], True)

            @pl.when(i == 0)
            def _():
                self.oa.start()
                self.ob.start()
            pl.when(i == 1)(self.w_hi.start)
            pl.when(i == 2)(self.t_lo.start)
        loop(4, mine)

    def middle(self):
        self.oa.wait_recv()
        self.kept[W, self.lo] = self.kept[W, self.lo] + self.in_o[self.lo]
        self.w_lo.start()
        self.ob.wait_recv()
        self.kept[T, self.hi] = self.kept[T, self.hi] + self.in_o[self.hi]
        self.t_hi.start()

    def end(self):
        for copy in (self.w_hi, self.t_lo, self.w_lo, self.t_hi):
            copy.wait_recv()

    def result(self, here):
        return self.kept[OWN, here] + self.in_w[here] + self.in_t[here]

    def drain(self, slots=True):
        if slots:
            self.free_slots()
        for copy in (self.oa, self.ob, self.w_hi, self.t_lo, self.w_lo, self.t_hi):
            copy.wait_send()

    def free_slots(self):
        self.d2d(2).wait_send()
        self.d2d(3).wait_send()


ROW_TILE = 32


def inv_rms_of(tensor):
    return lax.rsqrt(jnp.mean(tensor * tensor, axis=-1, keepdims=True) + RMS_EPS)


def rms_norm(tensor):
    return tensor * inv_rms_of(tensor)


def rms_back(tensor, grad_in):
    inv_rms = inv_rms_of(tensor)
    return inv_rms * grad_in - tensor * (inv_rms * inv_rms * inv_rms) * jnp.mean(grad_in * tensor, axis=-1, keepdims=True)


def gelu_tanh(tensor):
    return jax.nn.gelu(tensor, approximate=True)


def mlp_kernel(layer, y1, dy2, y2_hbm, dy1_hbm, w1_hbm, w2_hbm, x2_out, dy1_out, dw1_hbm, dw2_hbm,
               w1, w2, u_all, c_all, act, hid, dpre, tmp, dw1, dw2,
               g_snd, g_kept, g_o, g_w, g_t, d_snd, d_kept, d_o, d_w, d_t,
               us, ur, cs, cr, gs, gr, ds, dr, local):
    rows, hidden = y1.shape
    cols = w1.shape[1]
    get_w1 = pltpu.make_async_copy(w1_hbm.at[layer], w1, local.at[0])
    get_w2 = pltpu.make_async_copy(w2_hbm.at[layer], w2, local.at[1])
    get_w1.start()
    get_w2.start()
    gu = Gather(u_all, us, ur)
    gc = Gather(c_all, cs, cr)

    def block_rows(block):
        return pl.ds(pl.multiple_of(block * rows, rows), rows)

    def norm_in(here):
        u_all[here] = rms_norm(y1[here]).astype(bf16)
    tiles(rows, ROW_TILE, norm_in)
    enter((CORE, NEAR_T, NEAR_W))
    gu.start()

    def cast_in(here):
        c_all[here] = dy2[here].astype(bf16)
    tiles(rows, ROW_TILE, cast_in)
    get_w1.wait()
    get_w2.wait()

    def up(block):
        here = block_rows(block)
        act[here] = dot(u_all[here], w1[...], NN)

        def body(i):
            some = pl.ds(pl.multiple_of(block * rows + i * ROW_TILE, ROW_TILE), ROW_TILE)
            hid[some] = gelu_tanh(act[some]).astype(bf16)
        loop(rows // ROW_TILE, body)

    def down(block):
        tmp[...] = dot(c_all[block_rows(block)], w2[...], NT)

        def body(i):
            some = pl.ds(pl.multiple_of(block * rows + i * ROW_TILE, ROW_TILE), ROW_TILE)
            _, pull = jax.vjp(gelu_tanh, act[some])
            dpre[some] = pull(tmp[pl.ds(pl.multiple_of(i * ROW_TILE, ROW_TILE), ROW_TILE)])[0].astype(bf16)
        loop(rows // ROW_TILE, body)

    def part_of(lhs, rhs, transposed):
        def part(block, out, accumulate):
            here = block_rows(block)

            def body(col):
                value = dot(lhs[here], rhs[col, :], NT) if transposed else dot(lhs[here], rhs[:, col], NN)
                out[:, col] = out[:, col] + value if accumulate else value
            tiles(hidden, 256, body)
        return part

    rs_g = Scatter(part_of(hid, w2, False), (g_snd, g_kept, g_o, g_w, g_t), gs, gr)
    rs_d = Scatter(part_of(dpre, w1, True), (d_snd, d_kept, d_o, d_w, d_t), ds, dr)

    gu.each_block(up, gc.start)

    def between():
        rs_g.begin()
    gc.each_block(down, between)
    rs_g.middle()
    rs_d.begin()
    rs_g.free_slots()
    get_y2 = pltpu.make_async_copy(y2_hbm, g_snd.at[0], local.at[2])
    get_dy1 = pltpu.make_async_copy(dy1_hbm, g_snd.at[1], local.at[3])
    get_y2.start()
    get_dy1.start()

    def body2(col):
        dw2[col, :] = dot(hid[:, col], c_all[...], TN)
    tiles(cols, 128, body2)
    put_dw2 = pltpu.make_async_copy(dw2, dw2_hbm, local.at[0])
    put_dw2.start()
    rs_d.middle()
    rs_g.end()
    get_y2.wait()

    def x2_body(here):
        x2_out[here] = g_snd[0, here] - rs_g.result(here)
    tiles(rows, ROW_TILE, x2_body)

    def body1(col):
        dw1[col, :] = dot(u_all[:, col], dpre[...], TN)
    tiles(hidden, 256, body1)
    put_dw1 = pltpu.make_async_copy(dw1, dw1_hbm, local.at[1])
    put_dw1.start()
    get_dy1.wait()
    rs_d.end()

    def dy1_body(here):
        dy1_out[here] = g_snd[1, here] + rms_back(y1[here], rs_d.result(here))
    tiles(rows, ROW_TILE, dy1_body)
    gu.drain()
    gc.drain()
    rs_g.drain(False)
    rs_d.drain()
    put_dw2.wait()
    put_dw1.wait()


def attn_kernel(layer, scale, x2, dy1, y1, dy2, wqkv_hbm, wo_hbm, x1_out, dx2_out, dwqkv, dwo,
                wq, wk, wv, wo_all, u_all, c_all, q_all, k_all, v_all, dctx, ctx, ctx_in, prob,
                a_snd, a_kept, a_o, a_w, a_t, b_snd, b_kept, b_o, b_w, b_t,
                us, ur, cs, cr, ws, wr, xs, xr, as_, ar, bs, br, local):
    rows, hidden = x2.shape
    width = wq.shape[0]
    head = width // 2
    pos = 32
    n_seq = rows // pos
    gets = []
    for n in range(2):
        for j, ref in enumerate((wq, wk, wv)):
            gets.append(pltpu.make_async_copy(wqkv_hbm.at[layer, n, j], ref.at[pl.ds(n * head, head)], local.at[len(gets)]))
    gets.append(pltpu.make_async_copy(wo_hbm.at[layer], wo_all.at[pl.ds(0, width)], local.at[len(gets)]))
    for copy in gets:
        copy.start()
    gu = Gather(u_all, us, ur)
    gc = Gather(c_all, cs, cr)
    gw = Gather(wo_all, ws, wr)
    lanes = lax.broadcasted_iota(jnp.int32, (1, width), 1)
    masks = [(lanes < head), (lanes >= head)]

    def norm_in(here):
        u_all[here] = rms_norm(x2[here]).astype(bf16)
    tiles(rows, ROW_TILE, norm_in)
    enter(XOR[1:])
    gu.start()

    def cast_in(here):
        c_all[here] = dy1[here].astype(bf16)
    tiles(rows, ROW_TILE, cast_in)
    for copy in gets:
        copy.wait()

    def block_rows(block):
        return pl.ds(pl.multiple_of(block * rows, rows), rows)

    def pick(value, n):
        return jnp.where(masks[n], value, jnp.zeros_like(value))

    def qkv(block):
        here = block_rows(block)
        value = u_all[here]
        for weight, out in ((wq, q_all), (wk, k_all), (wv, v_all)):
            out[here] = dot(value, weight[...], NT).astype(bf16)

    def d_ctx(block):
        here = block_rows(block)
        dctx[here] = dot(c_all[here], wo_all[pl.ds(0, width)], NT).astype(bf16)

    def seq_get(ref, seq):
        return jnp.concatenate([ref[pl.ds(pl.multiple_of(b * rows + seq * pos, pos), pos)] for b in range(8)], axis=0)

    def seq_put(ref, seq, value):
        for b in range(8):
            ref[pl.ds(pl.multiple_of(b * rows + seq * pos, pos), pos)] = value[b * pos:(b + 1) * pos]

    def forward(seq):
        q, k, v = seq_get(q_all, seq), seq_get(k_all, seq), seq_get(v_all, seq)
        total = None
        for n in range(2):
            scores = dot(pick(q, n), k, NT) * scale
            expd = jnp.exp(scores - jnp.max(scores, axis=-1, keepdims=True))
            p = expd / jnp.sum(expd, axis=-1, keepdims=True)
            prob[2 * seq + n] = p
            out = dot(p.astype(bf16), pick(v, n), NN)
            total = out if total is None else total + out
        seq_put(ctx, seq, total.astype(bf16))

    def backward(seq):
        q, k, v, do = seq_get(q_all, seq), seq_get(k_all, seq), seq_get(v_all, seq), seq_get(dctx, seq)
        sums = [None, None, None]
        for n in range(2):
            p = prob[2 * seq + n]
            dp = dot(pick(do, n), v, NT)
            d_value = dot(p.astype(bf16), pick(do, n), TN)
            dsc = (p * (dp - jnp.sum(dp * p, axis=-1, keepdims=True)) * scale).astype(bf16)
            terms = [dot(dsc, pick(k, n), NN), dot(dsc, pick(q, n), TN), d_value]
            sums = [b if a is None else a + b for a, b in zip(sums, terms)]
        for ref, value in zip((q_all, k_all, v_all), sums):
            seq_put(ref, seq, value.astype(bf16))

    half = rows // 2

    def part_of(chunk):
        def part(block, out, accumulate):
            here = pl.ds(pl.multiple_of(block * rows + chunk * half, half), half)

            def body(col):
                value = dot(q_all[here], wq[:, col], NN) + dot(k_all[here], wk[:, col], NN) + dot(v_all[here], wv[:, col], NN)
                out[:, col] = out[:, col] + value if accumulate else value
            tiles(hidden, 256, body)
        return part

    rs_a = Scatter(part_of(0), (a_snd, a_kept, a_o, a_w, a_t), as_, ar)
    rs_b = Scatter(part_of(1), (b_snd, b_kept, b_o, b_w, b_t), bs, br)
    shares = [remote(ctx.at[pl.ds(b * rows, rows)], ctx_in.at[b], xs, xr, b - 1, XOR[b]) for b in range(1, 8)]

    gu.each_block(qkv, gc.start)
    loop(n_seq // 2, forward)
    gc.forward()
    loop(n_seq // 2, lambda i: forward(i + n_seq // 2))
    for copy in shares:
        copy.start()
    gw.start()
    gc.each_block(d_ctx, forwarded=True)
    loop(n_seq // 2, backward)
    gw.forward()
    rs_a.begin()
    loop(n_seq // 2, lambda i: backward(i + n_seq // 2))
    rs_a.middle()
    rs_b.begin()
    dwo[...] = dot(ctx[...], c_all[...], TN)
    gw.finish()
    for i, ref in enumerate((q_all, k_all, v_all)):
        grad = dot(ref[...], u_all[...], TN)
        for n in range(2):
            dwqkv[n, i] = grad[n * head:(n + 1) * head]
    rs_b.middle()
    for copy in shares:
        copy.wait_recv()
    for copy in (gw.p, gw.tp, gw.wp):
        copy.wait_recv()
    gw.last()

    def f_body(col):
        total = dot(ctx[pl.ds(0, rows)], wo_all[pl.ds(0, width), col], NN)
        for b in range(1, 8):
            total = total + dot(ctx_in[b], wo_all[pl.ds(b * width, width), col], NN)
        x1_out[:, col] = y1[:, col] - total
    tiles(hidden, 256, f_body)
    for chunk, item in enumerate((rs_a, rs_b)):
        item.end()

        def dx_body(i):
            part_rows = pl.ds(pl.multiple_of(i * ROW_TILE, ROW_TILE), ROW_TILE)
            here = pl.ds(pl.multiple_of(chunk * half + i * ROW_TILE, ROW_TILE), ROW_TILE)
            dx2_out[here] = dy2[here] + rms_back(x2[here], item.result(part_rows))
        loop(half // ROW_TILE, dx_body)
    for item in (gu, gc, gw, rs_a, rs_b):
        item.drain()
    for copy in shares:
        copy.wait_send()


def vmem(shape, dtype):
    return pltpu.VMEM(shape, dtype)


def scatter_scratch(rows, hidden):
    return [vmem((2, rows, hidden), f32), vmem((4, rows, hidden), f32)] + [vmem((rows, hidden), f32)] * 3


def sems(count):
    return [pltpu.SemaphoreType.DMA((count,))] * 2


def call(kernel, outs, scratch, collective_id, name, flops, near, far):
    inside, outside = pl.BlockSpec(memory_space=pltpu.VMEM), pl.BlockSpec(memory_space=pl.ANY)
    return pl.pallas_call(
        kernel,
        out_shape=[jax.ShapeDtypeStruct(shape, f32) for shape, _ in outs],
        in_specs=[inside] * len(near) + [outside] * len(far),
        out_specs=[inside if kept else outside for _, kept in outs],
        scratch_shapes=scratch,
        name=name,
        cost_estimate=pl.CostEstimate(flops=flops, bytes_accessed=10 ** 7, transcendentals=0),
        compiler_params=pltpu.CompilerParams(
            collective_id=collective_id, has_side_effects=True, vmem_limit_bytes=67043328),
    )(*near, *far)


def mlp_block(layer, y1, dy2, y2, dy1, w1, w2):
    rows, hidden = y1.shape
    cols = w1.shape[2]
    total = 8 * rows
    scratch = [vmem((hidden, cols), bf16), vmem((cols, hidden), bf16)]
    scratch += [vmem((total, hidden), bf16)] * 2 + [vmem((total, cols), f32)] + [vmem((total, cols), bf16)] * 2
    scratch += [vmem((rows, cols), f32), vmem((hidden, cols), f32), vmem((cols, hidden), f32)]
    scratch += scatter_scratch(rows, hidden) * 2 + sems(AG_SEMS) * 2 + sems(RS_SEMS) * 2 + sems(4)[:1]
    outs = [((rows, hidden), True)] * 2 + [((hidden, cols), False), ((cols, hidden), False)]
    kernel = functools.partial(mlp_kernel, layer)
    return call(kernel, outs, scratch, 2 * layer, "mlp_block", 12 * total * hidden * cols, (y1, dy2), (y2, dy1, w1, w2))


def attn_block(layer, scale, x2, dy1, y1, dy2, wqkv, wo):
    rows, hidden = x2.shape
    _, heads, _, head, _ = wqkv.shape
    width = heads * head
    total = 8 * rows
    scratch = [vmem((width, hidden), bf16)] * 3 + [vmem((8 * width, hidden), bf16)] + [vmem((total, hidden), bf16)] * 2
    scratch += [vmem((total, width), bf16)] * 5 + [vmem((8, rows, width), bf16), vmem((16, 256, 256), f32)]
    scratch += scatter_scratch(rows // 2, hidden) * 2 + sems(AG_SEMS) * 3 + sems(7) + sems(RS_SEMS) * 2 + sems(7)[:1]
    outs = [((rows, hidden), True)] * 2 + [((heads, 3, head, hidden), True), ((width, hidden), True)]
    kernel = functools.partial(attn_kernel, layer, scale)
    return call(kernel, outs, scratch, 2 * layer + 1, "attn_block", 24 * total * hidden * width, (x2, dy1, y1, dy2), (wqkv, wo))


def local_backward(y_one, y_two, dy_one, dy_two, w_qkv, w_out, w_up, w_down):
    n_layers, hidden, heads, _, head_dim = w_qkv.shape
    state_shape = y_one.shape
    y_one, y_two, dy_one, dy_two = [x.reshape(-1, hidden) for x in (y_one, y_two, dy_one, dy_two)]
    w_qkv = w_qkv.transpose(0, 2, 3, 4, 1)
    w_out = w_out.reshape(n_layers, heads * head_dim, hidden)
    grads = []
    for layer in reversed(range(n_layers)):
        y_two, dy_one, dw_up, dw_down = mlp_block(layer, y_one, dy_two, y_two, dy_one, w_up, w_down)
        y_one, dy_two, dw_qkv, dw_out = attn_block(layer, head_dim ** -0.5, y_two, dy_one, y_one, dy_two, w_qkv, w_out)
        grads.append((dw_qkv, dw_out.reshape(heads, head_dim, hidden), dw_up, dw_down))
    d_qkv, d_out, d_up, d_down = [jnp.stack(g) for g in zip(*grads[::-1])]
    state = [x.reshape(state_shape) for x in (y_one, y_two, dy_one, dy_two)]
    return (*state, d_qkv.transpose(0, 4, 1, 2, 3), d_out, d_up, d_down)


def solution(mesh):
    state_spec = P("dp", "tp", None)
    in_specs = (state_spec, state_spec, state_spec, state_spec, P(None, None, "tp", None, None), P(None, "tp", None, None), P(None, None, "tp"), P(None, "tp", None))
    out_specs = (state_spec, state_spec, state_spec, state_spec, P("dp", None, "tp", None, None), P("dp", "tp", None, None), P("dp", None, "tp"), P("dp", "tp", None))
    return jax.shard_map(local_backward, mesh=mesh, in_specs=in_specs, out_specs=out_specs, check_vma=False)
```

time: 859 us -> 557 us (0.65)
  waiting for transfers between devices: 578 us -> 0 us
  Pallas kernels: 0 us -> 533 us
  matrix products: 188 us -> 0 us
  other arithmetic: 45.7 us -> 16.7 us
  local copies, waits for them, and re-layouts: 22.9 us -> 4.98 us
  between operations: 15.1 us -> 0.7 us
    pallas_call x0 -> x4, Pallas kernels: none -> 533 us  [call(): pl.pallas_call(kernel, out_shape=[jax.ShapeDtypeStruct(shape, f32) for sh...]
    reduce_scatter x8 -> x0, waiting for transfers between devices: 378 us -> none  [scatter_positions(): return lax.psum_scatter(tensor, 'tp', scatter_dimension=1, tiled=True)]
    all_gather x8 -> x0, waiting for transfers between devices: 199 us -> none  [gather_positions(): return lax.all_gather(tensor, 'tp', axis=1, tiled=True)]
    dot_general x36 -> x0, matrix products: 188 us -> none  [the longest x2 19.2 us: local_backward(): jnp.einsum('bsh,fh->bsf', cot_mlp, wd_layer, preferred_element_type=jnp.f...]
    convert_element_type x8 -> x0, other arithmetic: 18.5 us -> none  [the longest x2 8.01 us: local_backward(): cot_att = gather_positions(dy_one.astype(jnp.bfloat16))]
    unnamed x103 -> x18, local copies, waits for them, and re-layouts: 20 us -> 4.98 us
    reduce_sum x6 -> x0, other arithmetic: 9.04 us -> none  [the longest x4 6.03 us: rms_back(): jnp.mean(grad_in * tensor, axis=-1, keepdims=True)]
  transfers between devices with their start and end apart: 16 -> 0, of which waited for: 15 -> 0; matrix products, arithmetic and copies ran while one was open for 20% -> 0% of each run, Pallas kernels for 0% -> 0%
where the time goes in v2:
time: 557 us; the launch traced here: 555 us
  Pallas kernels  533 us (96%)
  other arithmetic  16.7 us (3%)
    pallas_call x4, Pallas kernels, call(): pl.pallas_call(kernel, out_shape=[jax.ShapeDtypeStruct(shape, f32) for sh...  533 us
    another operation x3, other arithmetic, local_backward(): d_qkv, d_out, d_up, d_down = [jnp.stack(g) for g in zip(*grads[::-1])]  12.3 us

profile of v2, /device:TPU:81, one launch (start us, length us, event | category | flops | bytes accessed | tf_op | source)
XLA Modules:
  0.0 555.5 jit_solution(6750222790311859123)
XLA Ops:
  0.6 140.7 %mlp_block.2 = (f32[256,1280]{1,0:T(8,128)}, f32[256,1280]{1,0:T(8,128)}, f32[1280,640]{1,0:T(8,128)}, f32[640,1280]{1,0:T(8,128)}) custom-call(f32[256,1280]{1,0:T(8,128)} %bitcast.36, f32[256,1280]{1,0:T(8,128)} %bitcast.38, f32[256,1280]{1,0:T(8,128)} %bitcast.34, f32[256,1280]{1,0:T(8,128)} %bitcast.35, bf16[2,1280,640]{2,1,0:T(8,128)(2,1)} %w1_hbm.3, ...), custom_call_target="tpu_custom_call" | custom-call | flops 20132659200 | bytes 10000000 | tf_op jit(solution)/shard_map/mlp_block/pallas_call | solution.py:464
  141.4 127.1 %attn_block.2 = (f32[256,1280]{1,0:T(8,128)}, f32[256,1280]{1,0:T(8,128)}, f32[2,3,80,1280]{3,2,1,0:T(8,128)}, f32[160,1280]{1,0:T(8,128)}) custom-call(f32[256,1280]{1,0:T(8,128)} %get-tuple-element.24.x2.y2_hbm, f32[256,1280]{1,0:T(8,128)} %get-tuple-element.25.dy1.dy1_hbm, f32[256,1280]{1,0:T(8,128)} %bitcast.37, f32[256,1280]{1,0:T(8,128)} %bitcast.39, ...), custom_call_target="tpu_custom_call" | custom-call | flops 10066329600 | bytes 10000000 | tf_op jit(solution)/shard_map/attn_block/pallas_call | solution.py:464
  268.4 137.2 %mlp_block.3 = (f32[256,1280]{1,0:T(8,128)}, f32[256,1280]{1,0:T(8,128)}, f32[1280,640]{1,0:T(8,128)}, f32[640,1280]{1,0:T(8,128)}) custom-call(f32[256,1280]{1,0:T(8,128)} %get-tuple-element.26.y1, f32[256,1280]{1,0:T(8,128)} %get-tuple-element.27.dy2, f32[256,1280]{1,0:T(8,128)} %get-tuple-element.24.x2.y2_hbm, f32[256,1280]{1,0:T(8,128)} %get-tuple-element.25.dy1.dy1_hbm, ...), custom_call_target="tpu_custom_call" | custom-call | flops 20132659200 | bytes 10000000 | tf_op jit(solution)/shard_map/mlp_block/pallas_call | solution.py:464
  405.6 0.0 copy-start
  405.7 0.0 copy-start.1
  405.7 6.3 %pad_maximum_fusion = f32[2,1280,640]{2,1,0:T(8,128)} fusion(f32[1,1280,640]{2,1,0:T(8,128)} %bitcast.21, f32[1,1280,640]{2,1,0:T(8,128)} %bitcast.23), kind=kLoop, calls=%fused_computation | loop fusion | flops 1638400 | bytes 13107200 | tf_op jit(solution)/shard_map/stack | solution.py:514
  411.9 0.0 copy-done
  411.9 0.0 copy-done.1
  411.9 3.2 pad_maximum_fusion.1
  415.2 128.1 %attn_block.3 = (f32[256,1280]{1,0:T(8,128)}, f32[256,1280]{1,0:T(8,128)}, f32[2,3,80,1280]{3,2,1,0:T(8,128)}, f32[160,1280]{1,0:T(8,128)}) custom-call(f32[256,1280]{1,0:T(8,128)} %get-tuple-element.28.x2, f32[256,1280]{1,0:T(8,128)} %get-tuple-element.29.dy1, f32[256,1280]{1,0:T(8,128)} %get-tuple-element.26.y1, f32[256,1280]{1,0:T(8,128)} %get-tuple-element.27.dy2, ...), custom_call_target="tpu_custom_call" | custom-call | flops 10066329600 | bytes 10000000 | tf_op jit(solution)/shard_map/attn_block/pallas_call | solution.py:464
  543.3 0.0 copy-start.2
  543.3 2.9 pad_maximum_fusion.2
  546.1 0.0 copy-done.2
  546.1 0.0 copy-start.6
  546.1 4.4 maximum_bitcast_fusion
  550.5 0.0 copy-done.6
  550.5 0.0 copy-start.4
  550.5 1.1 copy.20
  551.6 0.7 copy-done.4
  552.3 1.1 copy.21
  553.3 0.0 copy-done.3
  553.3 1.1 copy.22
  554.4 0.0 copy-done.5
  554.4 1.1 copy.23
  (2 shorter events, 0.0 us)
Async XLA Ops:
  405.6 6.3 %copy-start = (f32[640,1280]{1,0:T(8,128)S(1)}, f32[640,1280]{1,0:T(8,128)}, u32[]{:S(2)}) copy-start(f32[640,1280]{1,0:T(8,128)} %get-tuple-element.39) | copy-start | bytes 9830404
  405.7 6.3 %copy-start.1 = (f32[640,1280]{1,0:T(8,128)S(1)}, f32[640,1280]{1,0:T(8,128)}, u32[]{:S(2)}) copy-start(f32[640,1280]{1,0:T(8,128)} %get-tuple-element.38) | copy-start | bytes 9830404
  543.3 2.9 copy-start.2
  546.1 4.4 copy-start.6
  550.5 1.8 copy-start.4
  550.5 2.8 copy-start.3
  552.3 2.1 copy-start.5

commit v3 on v2

--- a/solution.py
+++ b/solution.py
@@ -14,8 +14,8 @@
 OWN, T, W, O, PC, TP, WP, OP = range(8)
 XOR = (0, 6, 2, 4, 1, 7, 3, 5)
 CORE, NEAR_T, NEAR_W = 1, 6, 2
-AG_SEMS = 9
-RS_SEMS = 10
+AG_SEMS = 11
+RS_SEMS = 12
 NN, NT, TN = ((1,), (0,)), ((1,), (1,)), ((0,), (0,))
 
 
@@ -27,11 +27,13 @@
     return {"tp": out}
 
 
-def enter(masks):
-    barrier = pltpu.get_barrier_semaphore()
+def greet(masks):
     for mask in masks:
-        pl.semaphore_signal(barrier, inc=1, device_id=peer(mask), device_id_type=pl.DeviceIdType.MESH)
-    pl.semaphore_wait(barrier, len(masks))
+        pl.semaphore_signal(pltpu.get_barrier_semaphore(), inc=1, device_id=peer(mask), device_id_type=pl.DeviceIdType.MESH)
+
+
+def meet(masks):
+    pl.semaphore_wait(pltpu.get_barrier_semaphore(), len(masks))
 
 
 def remote(src, dst, send, recv, index, mask):
@@ -63,8 +65,10 @@
         def at(block, lo=0, size=rows):
             return buf.at[pl.ds(block * rows + lo, size)]
 
-        self.t = remote(at(OWN), at(T), send, recv, 0, NEAR_T)
-        self.w = remote(at(OWN), at(W), send, recv, 1, NEAR_W)
+        self.t_hi = remote(at(OWN, half, half), at(T, half, half), send, recv, 0, NEAR_T)
+        self.t_lo = remote(at(OWN, 0, half), at(T, 0, half), send, recv, 9, NEAR_T)
+        self.w_lo = remote(at(OWN, 0, half), at(W, 0, half), send, recv, 1, NEAR_W)
+        self.w_hi = remote(at(OWN, half, half), at(W, half, half), send, recv, 10, NEAR_W)
         self.p = remote(at(OWN), at(PC), send, recv, 2, CORE)
         self.oa = remote(at(W, 0, half), at(O, 0, half), send, recv, 3, NEAR_T)
         self.ob = remote(at(T, half, half), at(O, half, half), send, recv, 4, NEAR_W)
@@ -74,16 +78,19 @@
         self.opb = remote(at(O, half, half), at(OP, half, half), send, recv, 8, CORE)
 
     def start(self):
-        self.t.start()
-        self.w.start()
-        self.p.start()
+        for copy in (self.t_hi, self.w_lo, self.t_lo, self.w_hi, self.p):
+            copy.start()
 
     def forward(self):
-        self.t.wait_recv()
+        self.t_hi.wait_recv()
         self.ob.start()
+        self.w_lo.wait_recv()
+        self.oa.start()
+
+    def share(self):
+        self.t_lo.wait_recv()
         self.tp.start()
-        self.w.wait_recv()
-        self.oa.start()
+        self.w_hi.wait_recv()
         self.wp.start()
 
     def finish(self):
@@ -97,17 +104,13 @@
         self.opb.wait_recv()
 
     def drain(self):
-        for copy in (self.t, self.w, self.p, self.oa, self.ob, self.tp, self.wp, self.opa, self.opb):
+        for copy in (self.t_hi, self.t_lo, self.w_lo, self.w_hi, self.p, self.oa, self.ob, self.tp, self.wp, self.opa, self.opb):
             copy.wait_send()
 
-    def each_block(self, compute, after_forward=None, forwarded=False):
+    def each_block(self, compute, neighbours=None):
         def body(step):
-            if not forwarded:
-                @pl.when(step == 2)
-                def _():
-                    self.forward()
-                    if after_forward is not None:
-                        after_forward()
+            if neighbours is not None:
+                pl.when(step == 2)(neighbours)
             for when, act in ((1, self.p.wait_recv), (3, self.tp.wait_recv), (5, self.wp.wait_recv), (6, self.finish), (7, self.last)):
                 pl.when(step == when)(act)
             compute(step // 2 + 4 * lax.rem(step, 2))
@@ -125,22 +128,31 @@
         self.ob = remote(self.kept.at[O, hi], self.in_o.at[hi], send, recv, 5, NEAR_W)
         self.w_hi = remote(self.kept.at[W, hi], self.in_w.at[hi], send, recv, 6, NEAR_W)
         self.t_lo = remote(self.kept.at[T, lo], self.in_t.at[lo], send, recv, 7, NEAR_T)
-        self.w_lo = remote(self.kept.at[W, lo], self.in_w.at[lo], send, recv, 8, NEAR_W)
-        self.t_hi = remote(self.kept.at[T, hi], self.in_t.at[hi], send, recv, 9, NEAR_T)
+        quarter = half // 2
+        self.quarter, self.half = quarter, half
+        self.w_rows = [pl.ds(i * quarter, quarter) for i in range(2)]
+        self.t_rows = [pl.ds(half + i * quarter, quarter) for i in range(2)]
+        self.w_lo = [remote(self.kept.at[W, r], self.in_w.at[r], send, recv, 8 + i, NEAR_W) for i, r in enumerate(self.w_rows)]
+        self.t_hi = [remote(self.kept.at[T, r], self.in_t.at[r], send, recv, 10 + i, NEAR_T) for i, r in enumerate(self.t_rows)]
 
     def d2d(self, i):
         return remote(self.snd.at[lax.rem(i, 2)], self.kept.at[3 - i], self.send, self.recv, i, CORE)
 
     def begin(self):
-        def theirs(i):
+        self.theirs()
+        self.mine()
+
+    def theirs(self):
+        def body(i):
             @pl.when(i >= 2)
             def _():
                 self.d2d(i - 2).wait_send()
             self.part(7 - i, self.snd.at[lax.rem(i, 2)], False)
             self.d2d(i).start()
-        loop(4, theirs)
-
-        def mine(i):
+        loop(4, body)
+
+    def mine(self):
+        def body(i):
             self.d2d(i).wait_recv()
             self.part(3 - i, self.kept.at[3 - i], True)
 
@@ -150,27 +162,35 @@
                 self.ob.start()
             pl.when(i == 1)(self.w_hi.start)
             pl.when(i == 2)(self.t_lo.start)
-        loop(4, mine)
+        loop(4, body)
 
     def middle(self):
         self.oa.wait_recv()
-        self.kept[W, self.lo] = self.kept[W, self.lo] + self.in_o[self.lo]
-        self.w_lo.start()
+        for rows, copy in zip(self.w_rows, self.w_lo):
+            self.kept[W, rows] = self.kept[W, rows] + self.in_o[rows]
+            copy.start()
         self.ob.wait_recv()
-        self.kept[T, self.hi] = self.kept[T, self.hi] + self.in_o[self.hi]
-        self.t_hi.start()
-
-    def end(self):
-        for copy in (self.w_hi, self.t_lo, self.w_lo, self.t_hi):
-            copy.wait_recv()
-
-    def result(self, here):
-        return self.kept[OWN, here] + self.in_w[here] + self.in_t[here]
+        for rows, copy in zip(self.t_rows, self.t_hi):
+            self.kept[T, rows] = self.kept[T, rows] + self.in_o[rows]
+            copy.start()
+
+    def each_tile(self, apply):
+        self.w_hi.wait_recv()
+        self.t_lo.wait_recv()
+        for i in range(2):
+            self.w_lo[i].wait_recv()
+            self.t_hi[i].wait_recv()
+            for base in (i * self.quarter, self.half + i * self.quarter):
+                def body(k):
+                    start = pl.multiple_of(base + k * ROW_TILE, ROW_TILE)
+                    here = pl.ds(start, ROW_TILE)
+                    apply(start, self.kept[OWN, here] + self.in_w[here] + self.in_t[here])
+                loop(self.quarter // ROW_TILE, body)
 
     def drain(self, slots=True):
         if slots:
             self.free_slots()
-        for copy in (self.oa, self.ob, self.w_hi, self.t_lo, self.w_lo, self.t_hi):
+        for copy in (self.oa, self.ob, self.w_hi, self.t_lo, *self.w_lo, *self.t_hi):
             copy.wait_send()
 
     def free_slots(self):
@@ -198,31 +218,46 @@
     return jax.nn.gelu(tensor, approximate=True)
 
 
-def mlp_kernel(layer, y1, dy2, y2_hbm, dy1_hbm, w1_hbm, w2_hbm, x2_out, dy1_out, dw1_hbm, dw2_hbm,
-               w1, w2, u_all, c_all, act, hid, dpre, tmp, dw1, dw2,
+def mlp_kernel(layer, n_held, *refs):
+    mlp_body(layer, *refs[:6], *refs[6 + n_held:])
+
+
+def mlp_body(layer, y1_hbm, dy2_hbm, y2_hbm, dy1_hbm, w1_hbm, w2_hbm, x2_out, dy1_out, dw1_hbm, dw2_hbm,
+             y1, w1, w2, u_all, c_all, act, hid, dpre, tmp, dw1, dw2,
                g_snd, g_kept, g_o, g_w, g_t, d_snd, d_kept, d_o, d_w, d_t,
                us, ur, cs, cr, gs, gr, ds, dr, local):
     rows, hidden = y1.shape
     cols = w1.shape[1]
+    near = (CORE, NEAR_T, NEAR_W)
+    greet(near)
+    get_y1 = pltpu.make_async_copy(y1_hbm, y1, local.at[2])
+    get_dy2 = pltpu.make_async_copy(dy2_hbm, dy1_out, local.at[3])
+    get_y2 = pltpu.make_async_copy(y2_hbm, x2_out, local.at[4])
+    get_dy1 = pltpu.make_async_copy(dy1_hbm, dy1_out, local.at[5])
     get_w1 = pltpu.make_async_copy(w1_hbm.at[layer], w1, local.at[0])
     get_w2 = pltpu.make_async_copy(w2_hbm.at[layer], w2, local.at[1])
-    get_w1.start()
-    get_w2.start()
+    for copy in (get_y1, get_dy2, get_w1, get_w2, get_y2):
+        copy.start()
     gu = Gather(u_all, us, ur)
     gc = Gather(c_all, cs, cr)
 
     def block_rows(block):
         return pl.ds(pl.multiple_of(block * rows, rows), rows)
+
+    get_y1.wait()
 
     def norm_in(here):
         u_all[here] = rms_norm(y1[here]).astype(bf16)
     tiles(rows, ROW_TILE, norm_in)
-    enter((CORE, NEAR_T, NEAR_W))
+    meet(near)
     gu.start()
 
+    get_dy2.wait()
+
     def cast_in(here):
-        c_all[here] = dy2[here].astype(bf16)
+        c_all[here] = dy1_out[here].astype(bf16)
     tiles(rows, ROW_TILE, cast_in)
+    get_dy1.start()
     get_w1.wait()
     get_w2.wait()
 
@@ -257,53 +292,59 @@
     rs_g = Scatter(part_of(hid, w2, False), (g_snd, g_kept, g_o, g_w, g_t), gs, gr)
     rs_d = Scatter(part_of(dpre, w1, True), (d_snd, d_kept, d_o, d_w, d_t), ds, dr)
 
-    gu.each_block(up, gc.start)
-
-    def between():
-        rs_g.begin()
-    gc.each_block(down, between)
+    def u_neighbours():
+        gu.forward()
+        gu.share()
+        gc.start()
+
+    def c_neighbours():
+        gc.share()
+        rs_g.mine()
+    gu.each_block(up, u_neighbours)
+    rs_g.theirs()
+    gc.forward()
+    gc.each_block(down, c_neighbours)
     rs_g.middle()
     rs_d.begin()
-    rs_g.free_slots()
-    get_y2 = pltpu.make_async_copy(y2_hbm, g_snd.at[0], local.at[2])
-    get_dy1 = pltpu.make_async_copy(dy1_hbm, g_snd.at[1], local.at[3])
-    get_y2.start()
-    get_dy1.start()
 
     def body2(col):
         dw2[col, :] = dot(hid[:, col], c_all[...], TN)
     tiles(cols, 128, body2)
-    put_dw2 = pltpu.make_async_copy(dw2, dw2_hbm, local.at[0])
+    put_dw2 = pltpu.make_async_copy(dw2, dw2_hbm.at[layer], local.at[0])
     put_dw2.start()
     rs_d.middle()
-    rs_g.end()
     get_y2.wait()
 
-    def x2_body(here):
-        x2_out[here] = g_snd[0, here] - rs_g.result(here)
-    tiles(rows, ROW_TILE, x2_body)
+    def x2_body(start, total):
+        here = pl.ds(start, ROW_TILE)
+        x2_out[here] = x2_out[here] - total
+    rs_g.each_tile(x2_body)
 
     def body1(col):
         dw1[col, :] = dot(u_all[:, col], dpre[...], TN)
     tiles(hidden, 256, body1)
-    put_dw1 = pltpu.make_async_copy(dw1, dw1_hbm, local.at[1])
+    put_dw1 = pltpu.make_async_copy(dw1, dw1_hbm.at[layer], local.at[1])
     put_dw1.start()
     get_dy1.wait()
-    rs_d.end()
-
-    def dy1_body(here):
-        dy1_out[here] = g_snd[1, here] + rms_back(y1[here], rs_d.result(here))
-    tiles(rows, ROW_TILE, dy1_body)
+
+    def dy1_body(start, total):
+        here = pl.ds(start, ROW_TILE)
+        dy1_out[here] = dy1_out[here] + rms_back(y1[here], total)
+    rs_d.each_tile(dy1_body)
     gu.drain()
     gc.drain()
-    rs_g.drain(False)
+    rs_g.drain()
     rs_d.drain()
     put_dw2.wait()
     put_dw1.wait()
 
 
-def attn_kernel(layer, scale, x2, dy1, y1, dy2, wqkv_hbm, wo_hbm, x1_out, dx2_out, dwqkv, dwo,
-                wq, wk, wv, wo_all, u_all, c_all, q_all, k_all, v_all, dctx, ctx, ctx_in, prob,
+def attn_kernel(layer, scale, n_held, *refs):
+    attn_body(layer, scale, *refs[:6], *refs[6 + n_held:])
+
+
+def attn_body(layer, scale, x2_hbm, dy1_hbm, y1_hbm, dy2_hbm, wqkv_hbm, wo_hbm, x1_out, dx2_out, dwqkv_hbm, dwo_hbm, x2, dwqkv, dwo,
+                wq, wk, wv, wo_all, u_all, c_all, q_all, k_all, v_all, dctx, ctx, packed, ctx_in, others_ctx, relay, prob,
                 a_snd, a_kept, a_o, a_w, a_t, b_snd, b_kept, b_o, b_w, b_t,
                 us, ur, cs, cr, ws, wr, xs, xr, as_, ar, bs, br, local):
     rows, hidden = x2.shape
@@ -311,6 +352,13 @@
     head = width // 2
     pos = 32
     n_seq = rows // pos
+    greet(XOR[1:])
+    get_x2 = pltpu.make_async_copy(x2_hbm, x2, local.at[7])
+    get_dy1 = pltpu.make_async_copy(dy1_hbm, dx2_out, local.at[8])
+    get_dy2 = pltpu.make_async_copy(dy2_hbm, dx2_out, local.at[9])
+    get_y1 = pltpu.make_async_copy(y1_hbm, x1_out, local.at[10])
+    get_x2.start()
+    get_dy1.start()
     gets = []
     for n in range(2):
         for j, ref in enumerate((wq, wk, wv)):
@@ -324,15 +372,21 @@
     lanes = lax.broadcasted_iota(jnp.int32, (1, width), 1)
     masks = [(lanes < head), (lanes >= head)]
 
+    get_x2.wait()
+
     def norm_in(here):
         u_all[here] = rms_norm(x2[here]).astype(bf16)
     tiles(rows, ROW_TILE, norm_in)
-    enter(XOR[1:])
+    meet(XOR[1:])
     gu.start()
 
+    get_dy1.wait()
+
     def cast_in(here):
-        c_all[here] = dy1[here].astype(bf16)
+        c_all[here] = dx2_out[here].astype(bf16)
     tiles(rows, ROW_TILE, cast_in)
+    get_dy2.start()
+    get_y1.start()
     for copy in gets:
         copy.wait()
 
@@ -398,19 +452,51 @@
 
     rs_a = Scatter(part_of(0), (a_snd, a_kept, a_o, a_w, a_t), as_, ar)
     rs_b = Scatter(part_of(1), (b_snd, b_kept, b_o, b_w, b_t), bs, br)
-    shares = [remote(ctx.at[pl.ds(b * rows, rows)], ctx_in.at[b], xs, xr, b - 1, XOR[b]) for b in range(1, 8)]
-
-    gu.each_block(qkv, gc.start)
+    shares = [remote(packed.at[b], ctx_in.at[b], xs, xr, i, XOR[b])
+              for i, b in enumerate((T, W, PC, TP, WP))]
+    via, onward = [], []
+    split = packed.shape[1] // 2
+    for i, (row, near, others) in enumerate(((0, NEAR_T, (2, 3)), (split, NEAR_W, (6, 7)))):
+        for j, b in enumerate((O, OP)):
+            slot = 2 * i + j
+            via.append(remote(packed.at[b, pl.ds(row, split)], relay.at[slot], xs, xr, 5 + slot, near))
+            onward.append(remote(relay.at[slot], ctx_in.at[b, pl.ds(row, split)], xs, xr, 9 + slot, others[j]))
+
+    def u_neighbours():
+        gu.forward()
+        gu.share()
+        gc.start()
+    gu.each_block(qkv, u_neighbours)
     loop(n_seq // 2, forward)
     gc.forward()
     loop(n_seq // 2, lambda i: forward(i + n_seq // 2))
-    for copy in shares:
+    extra = width - 128
+    group = rows * extra // 128
+
+    def pack(b):
+        value = ctx[block_rows(b)]
+        packed[b, pl.ds(0, rows)] = value[:, :128]
+        packed[b, pl.ds(rows, group)] = jnp.concatenate(
+            [value[i * group:(i + 1) * group, 128:] for i in range(rows // group)], axis=1)
+
+    def unpack(i):
+        b = i + 1
+        rest = ctx_in[b, pl.ds(rows, group)]
+        rest = jnp.concatenate([rest[:, j * extra:(j + 1) * extra] for j in range(rows // group)], axis=0)
+        others_ctx[b] = jnp.concatenate([ctx_in[b, pl.ds(0, rows)], rest], axis=1)
+    loop(8, pack)
+    gc.share()
+    for copy in via + shares:
         copy.start()
     gw.start()
-    gc.each_block(d_ctx, forwarded=True)
+    gc.each_block(d_ctx)
+    for first, second in zip(via, onward):
+        first.wait_recv()
+        second.start()
     loop(n_seq // 2, backward)
     gw.forward()
     rs_a.begin()
+    gw.share()
     loop(n_seq // 2, lambda i: backward(i + n_seq // 2))
     rs_a.middle()
     rs_b.begin()
@@ -420,31 +506,38 @@
         grad = dot(ref[...], u_all[...], TN)
         for n in range(2):
             dwqkv[n, i] = grad[n * head:(n + 1) * head]
+    puts = [pltpu.make_async_copy(dwqkv, dwqkv_hbm.at[layer], local.at[0]),
+            pltpu.make_async_copy(dwo, dwo_hbm.at[layer], local.at[1])]
+    for copy in puts:
+        copy.start()
     rs_b.middle()
-    for copy in shares:
+    for copy in shares + onward:
         copy.wait_recv()
     for copy in (gw.p, gw.tp, gw.wp):
         copy.wait_recv()
     gw.last()
 
+    loop(7, unpack)
+    get_y1.wait()
+
     def f_body(col):
         total = dot(ctx[pl.ds(0, rows)], wo_all[pl.ds(0, width), col], NN)
         for b in range(1, 8):
-            total = total + dot(ctx_in[b], wo_all[pl.ds(b * width, width), col], NN)
-        x1_out[:, col] = y1[:, col] - total
+            total = total + dot(others_ctx[b], wo_all[pl.ds(b * width, width), col], NN)
+        x1_out[:, col] = x1_out[:, col] - total
     tiles(hidden, 256, f_body)
+    get_dy2.wait()
     for chunk, item in enumerate((rs_a, rs_b)):
-        item.end()
-
-        def dx_body(i):
-            part_rows = pl.ds(pl.multiple_of(i * ROW_TILE, ROW_TILE), ROW_TILE)
-            here = pl.ds(pl.multiple_of(chunk * half + i * ROW_TILE, ROW_TILE), ROW_TILE)
-            dx2_out[here] = dy2[here] + rms_back(x2[here], item.result(part_rows))
-        loop(half // ROW_TILE, dx_body)
+        def dx_body(start, total):
+            here = pl.ds(pl.multiple_of(chunk * half + start, ROW_TILE), ROW_TILE)
+            dx2_out[here] = dx2_out[here] + rms_back(x2[here], total)
+        item.each_tile(dx_body)
     for item in (gu, gc, gw, rs_a, rs_b):
         item.drain()
-    for copy in shares:
+    for copy in shares + via + onward:
         copy.wait_send()
+    for copy in puts:
+        copy.wait()
 
 
 def vmem(shape, dtype):
@@ -459,45 +552,47 @@
     return [pltpu.SemaphoreType.DMA((count,))] * 2
 
 
-def call(kernel, outs, scratch, collective_id, name, flops, near, far):
+def call(kernel, outs, scratch, collective_id, name, flops, args, held):
     inside, outside = pl.BlockSpec(memory_space=pltpu.VMEM), pl.BlockSpec(memory_space=pl.ANY)
     return pl.pallas_call(
         kernel,
         out_shape=[jax.ShapeDtypeStruct(shape, f32) for shape, _ in outs],
-        in_specs=[inside] * len(near) + [outside] * len(far),
+        in_specs=[outside] * len(args + held),
+        input_output_aliases={len(args) + i: 2 + i for i in range(len(held))},
         out_specs=[inside if kept else outside for _, kept in outs],
         scratch_shapes=scratch,
         name=name,
         cost_estimate=pl.CostEstimate(flops=flops, bytes_accessed=10 ** 7, transcendentals=0),
         compiler_params=pltpu.CompilerParams(
             collective_id=collective_id, has_side_effects=True, vmem_limit_bytes=67043328),
-    )(*near, *far)
-
-
-def mlp_block(layer, y1, dy2, y2, dy1, w1, w2):
+    )(*args, *held)
+
+
+def mlp_block(layer, y1, dy2, y2, dy1, w1, w2, held):
     rows, hidden = y1.shape
     cols = w1.shape[2]
     total = 8 * rows
-    scratch = [vmem((hidden, cols), bf16), vmem((cols, hidden), bf16)]
+    scratch = [vmem((rows, hidden), f32), vmem((hidden, cols), bf16), vmem((cols, hidden), bf16)]
     scratch += [vmem((total, hidden), bf16)] * 2 + [vmem((total, cols), f32)] + [vmem((total, cols), bf16)] * 2
     scratch += [vmem((rows, cols), f32), vmem((hidden, cols), f32), vmem((cols, hidden), f32)]
-    scratch += scatter_scratch(rows, hidden) * 2 + sems(AG_SEMS) * 2 + sems(RS_SEMS) * 2 + sems(4)[:1]
-    outs = [((rows, hidden), True)] * 2 + [((hidden, cols), False), ((cols, hidden), False)]
-    kernel = functools.partial(mlp_kernel, layer)
-    return call(kernel, outs, scratch, 2 * layer, "mlp_block", 12 * total * hidden * cols, (y1, dy2), (y2, dy1, w1, w2))
-
-
-def attn_block(layer, scale, x2, dy1, y1, dy2, wqkv, wo):
+    scratch += scatter_scratch(rows, hidden) * 2 + sems(AG_SEMS) * 2 + sems(RS_SEMS) * 2 + sems(6)[:1]
+    outs = [((rows, hidden), True)] * 2 + [(w1.shape, False), (w2.shape, False)]
+    kernel = functools.partial(mlp_kernel, layer, len(held))
+    return call(kernel, outs, scratch, 2 * layer, "mlp_block", 12 * total * hidden * cols, (y1, dy2, y2, dy1, w1, w2), held)
+
+
+def attn_block(layer, scale, x2, dy1, y1, dy2, wqkv, wo, held):
     rows, hidden = x2.shape
     _, heads, _, head, _ = wqkv.shape
     width = heads * head
     total = 8 * rows
-    scratch = [vmem((width, hidden), bf16)] * 3 + [vmem((8 * width, hidden), bf16)] + [vmem((total, hidden), bf16)] * 2
-    scratch += [vmem((total, width), bf16)] * 5 + [vmem((8, rows, width), bf16), vmem((16, 256, 256), f32)]
-    scratch += scatter_scratch(rows // 2, hidden) * 2 + sems(AG_SEMS) * 3 + sems(7) + sems(RS_SEMS) * 2 + sems(7)[:1]
-    outs = [((rows, hidden), True)] * 2 + [((heads, 3, head, hidden), True), ((width, hidden), True)]
-    kernel = functools.partial(attn_kernel, layer, scale)
-    return call(kernel, outs, scratch, 2 * layer + 1, "attn_block", 24 * total * hidden * width, (x2, dy1, y1, dy2), (wqkv, wo))
+    scratch = [vmem((rows, hidden), f32), vmem((heads, 3, head, hidden), f32), vmem((width, hidden), f32)] + [vmem((width, hidden), bf16)] * 3 + [vmem((8 * width, hidden), bf16)] + [vmem((total, hidden), bf16)] * 2
+    scratch += [vmem((total, width), bf16)] * 5 + [vmem((8, rows * width // 128, 128), bf16)] * 2
+    scratch += [vmem((8, rows, width), bf16), vmem((4, rows * width // 256, 128), bf16), vmem((16, 256, 256), f32)]
+    scratch += scatter_scratch(rows // 2, hidden) * 2 + sems(AG_SEMS) * 3 + sems(13) + sems(RS_SEMS) * 2 + sems(11)[:1]
+    outs = [((rows, hidden), True)] * 2 + [(wqkv.shape, False), (wo.shape, False)]
+    kernel = functools.partial(attn_kernel, layer, scale, len(held))
+    return call(kernel, outs, scratch, 2 * layer + 1, "attn_block", 24 * total * hidden * width, (x2, dy1, y1, dy2, wqkv, wo), held)
 
 
 def local_backward(y_one, y_two, dy_one, dy_two, w_qkv, w_out, w_up, w_down):
@@ -506,14 +601,14 @@
     y_one, y_two, dy_one, dy_two = [x.reshape(-1, hidden) for x in (y_one, y_two, dy_one, dy_two)]
     w_qkv = w_qkv.transpose(0, 2, 3, 4, 1)
     w_out = w_out.reshape(n_layers, heads * head_dim, hidden)
-    grads = []
+    held_mlp, held_attn = (), ()
     for layer in reversed(range(n_layers)):
-        y_two, dy_one, dw_up, dw_down = mlp_block(layer, y_one, dy_two, y_two, dy_one, w_up, w_down)
-        y_one, dy_two, dw_qkv, dw_out = attn_block(layer, head_dim ** -0.5, y_two, dy_one, y_one, dy_two, w_qkv, w_out)
-        grads.append((dw_qkv, dw_out.reshape(heads, head_dim, hidden), dw_up, dw_down))
-    d_qkv, d_out, d_up, d_down = [jnp.stack(g) for g in zip(*grads[::-1])]
+        y_two, dy_one, *held_mlp = mlp_block(layer, y_one, dy_two, y_two, dy_one, w_up, w_down, tuple(held_mlp))
+        y_one, dy_two, *held_attn = attn_block(
+            layer, head_dim ** -0.5, y_two, dy_one, y_one, dy_two, w_qkv, w_out, tuple(held_attn))
+    d_qkv, d_out, d_up, d_down = *held_attn, *held_mlp
     state = [x.reshape(state_shape) for x in (y_one, y_two, dy_one, dy_two)]
-    return (*state, d_qkv.transpose(0, 4, 1, 2, 3), d_out, d_up, d_down)
+    return (*state, d_qkv.transpose(0, 4, 1, 2, 3), d_out.reshape(n_layers, heads, head_dim, hidden), d_up, d_down)
 
 
 def solution(mesh):

time: 557 us -> 514 us (0.923)
  Pallas kernels: 533 us -> 494 us
  other arithmetic: 16.7 us -> 0.01 us
  local copies, waits for them, and re-layouts: 4.98 us -> 19.6 us
    pallas_call x4, Pallas kernels: 533 us -> 494 us  [call(): pl.pallas_call(kernel, out_shape=[jax.ShapeDtypeStruct(shape, f32) for sh...]
    unnamed x18 -> x26, local copies, waits for them, and re-layouts: 4.98 us -> 19.6 us
    another operation x3 -> x0, other arithmetic: 12.3 us -> none  [local_backward(): d_qkv, d_out, d_up, d_down = [jnp.stack(g) for g in zip(*grads[::-1])]]
where the time goes in v3:
time: 514 us
  Pallas kernels  494 us (96%)
  local copies, waits for them, and re-layouts  19.6 us (4%)
    pallas_call x4, Pallas kernels, call(): pl.pallas_call(kernel, out_shape=[jax.ShapeDtypeStruct(shape, f32) for sh...  494 us
    unnamed x26, local copies, waits for them, and re-layouts  19.6 us

profile of v3, /device:TPU:81, one launch (start us, length us, event | category | flops | bytes accessed | tf_op | source)
XLA Modules:
  0.0 514.3 jit_solution(8721233304901574747)
XLA Ops:
  0.6 135.9 %mlp_block.2 = (f32[256,1280]{1,0:T(8,128)}, f32[256,1280]{1,0:T(8,128)}, f32[2,1280,640]{2,1,0:T(8,128)}, f32[2,640,1280]{2,1,0:T(8,128)}) custom-call(f32[256,1280]{1,0:T(8,128)} %bitcast.26, f32[256,1280]{1,0:T(8,128)} %bitcast.28, f32[256,1280]{1,0:T(8,128)} %bitcast.24, f32[256,1280]{1,0:T(8,128)} %bitcast.25, bf16[2,1280,640]{2,1,0:T(8,128)(2,1)} %refs_4_.3, ...), custom_call_target="tpu_custom_call" | custom-call | flops 20132659200 | bytes 10000000 | tf_op jit(solution)/shard_map/mlp_block/pallas_call | solution.py:557
  136.5 112.3 %attn_block.2 = (f32[256,1280]{1,0:T(8,128)}, f32[256,1280]{1,0:T(8,128)}, f32[2,2,3,80,1280]{4,3,2,1,0:T(8,128)}, f32[2,160,1280]{2,1,0:T(8,128)}) custom-call(f32[256,1280]{1,0:T(8,128)} %get-tuple-element.24.refs_0_.refs_2_, f32[256,1280]{1,0:T(8,128)} %get-tuple-element.25.refs_1_.refs_3_, f32[256,1280]{1,0:T(8,128)} %bitcast.27, f32[256,1280]{1,0:T(8,128)} %bitcast.29, ...), custom_call_target="tpu_custom_call" | custom-call | flops 10066329600 | bytes 10000000 | tf_op jit(solution)/shard_map/attn_block/pallas_call | solution.py:557
  248.8 133.4 %mlp_block.3 = (f32[256,1280]{1,0:T(8,128)}, f32[256,1280]{1,0:T(8,128)}, f32[2,1280,640]{2,1,0:T(8,128)}, f32[2,640,1280]{2,1,0:T(8,128)}) custom-call(f32[256,1280]{1,0:T(8,128)} %get-tuple-element.26.refs_0_.refs_2_, f32[256,1280]{1,0:T(8,128)} %get-tuple-element.27.refs_1_.refs_3_, ...), custom_call_target="tpu_custom_call", output_to_operand_aliasing={{2}: (6, {}), {3}: (7, {})} | custom-call | flops 20132659200 | bytes 10000000 | tf_op jit(solution)/shard_map/mlp_block/pallas_call | solution.py:557
  382.2 112.5 %attn_block.3 = (f32[256,1280]{1,0:T(8,128)}, f32[256,1280]{1,0:T(8,128)}, f32[2,2,3,80,1280]{4,3,2,1,0:T(8,128)}, f32[2,160,1280]{2,1,0:T(8,128)}) custom-call(f32[256,1280]{1,0:T(8,128)} %get-tuple-element.30.refs_0_, f32[256,1280]{1,0:T(8,128)} %get-tuple-element.31.refs_1_, ...), custom_call_target="tpu_custom_call", output_to_operand_aliasing={{2}: (6, {}), {3}: (7, {})} | custom-call | flops 10066329600 | bytes 10000000 | tf_op jit(solution)/shard_map/attn_block/pallas_call | solution.py:557
  494.7 0.0 copy-start.3
  494.7 2.6 copy.32
  497.3 0.0 copy-done.3
  497.3 0.0 copy-start.2
  497.3 0.0 copy-start.4
  497.3 1.1 copy.33
  498.3 0.7 copy-done.2
  499.1 1.1 copy.34
  500.1 0.0 copy-done.4
  500.1 1.1 copy.35
  501.2 1.3 copy-done
  502.5 2.5 copy.36
  505.0 0.5 copy-done.1
  505.6 1.2 copy.37
  506.7 0.0 slice-done
  506.7 0.1 slice-done.1
  506.8 3.3 copy.38
  510.1 0.0 slice-done.2
  510.1 1.4 slice-done.3
  511.5 2.8 copy.39
  (8 shorter events, 0.0 us)
Async XLA Ops:
  494.7 2.6 copy-start.3
  497.3 1.8 copy-start.2
  497.3 2.8 copy-start.4
  499.1 3.4 copy-start
  500.1 6.6 %slice-start = ((s8[6553600]{0:T(1024)(128)(4,1)}), s8[4194304]{0:T(1024)(128)(4,1)S(1)}, s32[]{:S(2)}) async-start(s8[6553600]{0:T(1024)(128)(4,1)} %bitcast.12), calls=%async_computation | async-start | bytes 8388608
  502.5 3.0 copy-start.1
  502.5 4.3 slice-start.1
  505.6 4.6 slice-start.2
  506.8 4.7 slice-start.3

commit v4 on v3

--- a/solution.py
+++ b/solution.py
@@ -174,7 +174,7 @@
             self.kept[T, rows] = self.kept[T, rows] + self.in_o[rows]
             copy.start()
 
-    def each_tile(self, apply):
+    def each_tile(self, apply, done=lambda index, start, size: None):
         self.w_hi.wait_recv()
         self.t_lo.wait_recv()
         for i in range(2):
@@ -186,6 +186,7 @@
                     here = pl.ds(start, ROW_TILE)
                     apply(start, self.kept[OWN, here] + self.in_w[here] + self.in_t[here])
                 loop(self.quarter // ROW_TILE, body)
+                done(2 * i + base // self.half, base, self.quarter)
 
     def drain(self, slots=True):
         if slots:
@@ -218,11 +219,13 @@
     return jax.nn.gelu(tensor, approximate=True)
 
 
-def mlp_kernel(layer, n_held, *refs):
-    mlp_body(layer, *refs[:6], *refs[6 + n_held:])
-
-
-def mlp_body(layer, y1_hbm, dy2_hbm, y2_hbm, dy1_hbm, w1_hbm, w2_hbm, x2_out, dy1_out, dw1_hbm, dw2_hbm,
+def mlp_kernel(layer, first, n_held, *refs):
+    count = 6 if first else 7
+    u_hbm = None if first else refs[6]
+    mlp_body(layer, u_hbm, *refs[:6], *refs[count + n_held:])
+
+
+def mlp_body(layer, u_hbm, y1_hbm, dy2_hbm, y2_hbm, dy1_hbm, w1_hbm, w2_hbm, x2_hbm, dy1_new, dw1_hbm, dw2_hbm, u_new, x2_out, dy1_out, u_out,
              y1, w1, w2, u_all, c_all, act, hid, dpre, tmp, dw1, dw2,
                g_snd, g_kept, g_o, g_w, g_t, d_snd, d_kept, d_o, d_w, d_t,
                us, ur, cs, cr, gs, gr, ds, dr, local):
@@ -236,6 +239,9 @@
     get_dy1 = pltpu.make_async_copy(dy1_hbm, dy1_out, local.at[5])
     get_w1 = pltpu.make_async_copy(w1_hbm.at[layer], w1, local.at[0])
     get_w2 = pltpu.make_async_copy(w2_hbm.at[layer], w2, local.at[1])
+    if u_hbm is not None:
+        get_u = pltpu.make_async_copy(u_hbm, u_all.at[pl.ds(0, rows)], local.at[6])
+        get_u.start()
     for copy in (get_y1, get_dy2, get_w1, get_w2, get_y2):
         copy.start()
     gu = Gather(u_all, us, ur)
@@ -244,11 +250,14 @@
     def block_rows(block):
         return pl.ds(pl.multiple_of(block * rows, rows), rows)
 
-    get_y1.wait()
-
-    def norm_in(here):
-        u_all[here] = rms_norm(y1[here]).astype(bf16)
-    tiles(rows, ROW_TILE, norm_in)
+    if u_hbm is None:
+        get_y1.wait()
+
+        def norm_in(here):
+            u_all[here] = rms_norm(y1[here]).astype(bf16)
+        tiles(rows, ROW_TILE, norm_in)
+    else:
+        get_u.wait()
     meet(near)
     gu.start()
 
@@ -314,11 +323,18 @@
     put_dw2.start()
     rs_d.middle()
     get_y2.wait()
+    if u_hbm is not None:
+        get_y1.wait()
 
     def x2_body(start, total):
         here = pl.ds(start, ROW_TILE)
-        x2_out[here] = x2_out[here] - total
+        x2 = x2_out[here] - total
+        x2_out[here] = x2
+        u_out[here] = rms_norm(x2).astype(bf16)
     rs_g.each_tile(x2_body)
+    puts = [pltpu.make_async_copy(x2_out, x2_hbm, local.at[2]), pltpu.make_async_copy(u_out, u_new, local.at[3])]
+    for copy in puts:
+        copy.start()
 
     def body1(col):
         dw1[col, :] = dot(u_all[:, col], dpre[...], TN)
@@ -330,20 +346,27 @@
     def dy1_body(start, total):
         here = pl.ds(start, ROW_TILE)
         dy1_out[here] = dy1_out[here] + rms_back(y1[here], total)
-    rs_d.each_tile(dy1_body)
+
+    def dy1_done(index, start, size):
+        here = pl.ds(start, size)
+        puts.append(pltpu.make_async_copy(dy1_out.at[here], dy1_new.at[here], local.at[7 + index]))
+        puts[-1].start()
+    rs_d.each_tile(dy1_body, dy1_done)
     gu.drain()
     gc.drain()
     rs_g.drain()
     rs_d.drain()
-    put_dw2.wait()
-    put_dw1.wait()
-
-
-def attn_kernel(layer, scale, n_held, *refs):
-    attn_body(layer, scale, *refs[:6], *refs[6 + n_held:])
-
-
-def attn_body(layer, scale, x2_hbm, dy1_hbm, y1_hbm, dy2_hbm, wqkv_hbm, wo_hbm, x1_out, dx2_out, dwqkv_hbm, dwo_hbm, x2, dwqkv, dwo,
+    for copy in (put_dw2, put_dw1, *puts):
+        copy.wait()
+
+
+def attn_kernel(layer, scale, last, n_held, *refs):
+    rest = refs[7 + n_held:]
+    outs = rest[:4] + ((None,) if last else rest[4:5])
+    attn_body(layer, scale, *refs[:7], *outs, *rest[4 if last else 5:])
+
+
+def attn_body(layer, scale, x2_hbm, dy1_hbm, y1_hbm, dy2_hbm, wqkv_hbm, wo_hbm, u_hbm, x1_hbm, dx2_hbm, dwqkv_hbm, dwo_hbm, u_new, x1_out, dx2_out, u_out, x2, dwqkv, dwo,
                 wq, wk, wv, wo_all, u_all, c_all, q_all, k_all, v_all, dctx, ctx, packed, ctx_in, others_ctx, relay, prob,
                 a_snd, a_kept, a_o, a_w, a_t, b_snd, b_kept, b_o, b_w, b_t,
                 us, ur, cs, cr, ws, wr, xs, xr, as_, ar, bs, br, local):
@@ -352,13 +375,15 @@
     head = width // 2
     pos = 32
     n_seq = rows // pos
-    greet(XOR[1:])
+    met = [XOR[b] for b in (T, W, PC, TP, WP)]
+    greet(met)
     get_x2 = pltpu.make_async_copy(x2_hbm, x2, local.at[7])
     get_dy1 = pltpu.make_async_copy(dy1_hbm, dx2_out, local.at[8])
     get_dy2 = pltpu.make_async_copy(dy2_hbm, dx2_out, local.at[9])
     get_y1 = pltpu.make_async_copy(y1_hbm, x1_out, local.at[10])
-    get_x2.start()
-    get_dy1.start()
+    get_u = pltpu.make_async_copy(u_hbm, u_all.at[pl.ds(0, rows)], local.at[11])
+    for copy in (get_u, get_dy1, get_x2):
+        copy.start()
     gets = []
     for n in range(2):
         for j, ref in enumerate((wq, wk, wv)):
@@ -372,12 +397,8 @@
     lanes = lax.broadcasted_iota(jnp.int32, (1, width), 1)
     masks = [(lanes < head), (lanes >= head)]
 
-    get_x2.wait()
-
-    def norm_in(here):
-        u_all[here] = rms_norm(x2[here]).astype(bf16)
-    tiles(rows, ROW_TILE, norm_in)
-    meet(XOR[1:])
+    get_u.wait()
+    meet(met)
     gu.start()
 
     get_dy1.wait()
@@ -526,12 +547,26 @@
             total = total + dot(others_ctx[b], wo_all[pl.ds(b * width, width), col], NN)
         x1_out[:, col] = x1_out[:, col] - total
     tiles(hidden, 256, f_body)
+    puts.append(pltpu.make_async_copy(x1_out, x1_hbm, local.at[2]))
+    puts[-1].start()
+    if u_new is not None:
+        def norm_out(here):
+            u_out[here] = rms_norm(x1_out[here]).astype(bf16)
+        tiles(rows, ROW_TILE, norm_out)
+        puts.append(pltpu.make_async_copy(u_out, u_new, local.at[3]))
+        puts[-1].start()
+    get_x2.wait()
     get_dy2.wait()
     for chunk, item in enumerate((rs_a, rs_b)):
         def dx_body(start, total):
             here = pl.ds(pl.multiple_of(chunk * half + start, ROW_TILE), ROW_TILE)
             dx2_out[here] = dx2_out[here] + rms_back(x2[here], total)
-        item.each_tile(dx_body)
+
+        def dx_done(index, start, size):
+            here = pl.ds(chunk * half + start, size)
+            puts.append(pltpu.make_async_copy(dx2_out.at[here], dx2_hbm.at[here], local.at[12 + 4 * chunk + index]))
+            puts[-1].start()
+        item.each_tile(dx_body, dx_done)
     for item in (gu, gc, gw, rs_a, rs_b):
         item.drain()
     for copy in shares + via + onward:
@@ -552,47 +587,51 @@
     return [pltpu.SemaphoreType.DMA((count,))] * 2
 
 
-def call(kernel, outs, scratch, collective_id, name, flops, args, held):
+def call(kernel, outs, scratch, collective_id, name, flops, limit, args, held):
     inside, outside = pl.BlockSpec(memory_space=pltpu.VMEM), pl.BlockSpec(memory_space=pl.ANY)
     return pl.pallas_call(
         kernel,
-        out_shape=[jax.ShapeDtypeStruct(shape, f32) for shape, _ in outs],
+        out_shape=[jax.ShapeDtypeStruct(shape, dtype) for shape, _, dtype in outs],
         in_specs=[outside] * len(args + held),
         input_output_aliases={len(args) + i: 2 + i for i in range(len(held))},
-        out_specs=[inside if kept else outside for _, kept in outs],
+        out_specs=[inside if kept else outside for _, kept, _ in outs],
         scratch_shapes=scratch,
         name=name,
         cost_estimate=pl.CostEstimate(flops=flops, bytes_accessed=10 ** 7, transcendentals=0),
         compiler_params=pltpu.CompilerParams(
-            collective_id=collective_id, has_side_effects=True, vmem_limit_bytes=67043328),
+            collective_id=collective_id, has_side_effects=True, vmem_limit_bytes=limit),
     )(*args, *held)
 
 
-def mlp_block(layer, y1, dy2, y2, dy1, w1, w2, held):
+def mlp_block(layer, u, y1, dy2, y2, dy1, w1, w2, held):
     rows, hidden = y1.shape
     cols = w1.shape[2]
     total = 8 * rows
-    scratch = [vmem((rows, hidden), f32), vmem((hidden, cols), bf16), vmem((cols, hidden), bf16)]
+    scratch = [vmem((rows, hidden), f32)] * 2 + [vmem((rows, hidden), bf16)]
+    scratch += [vmem((rows, hidden), f32), vmem((hidden, cols), bf16), vmem((cols, hidden), bf16)]
     scratch += [vmem((total, hidden), bf16)] * 2 + [vmem((total, cols), f32)] + [vmem((total, cols), bf16)] * 2
     scratch += [vmem((rows, cols), f32), vmem((hidden, cols), f32), vmem((cols, hidden), f32)]
-    scratch += scatter_scratch(rows, hidden) * 2 + sems(AG_SEMS) * 2 + sems(RS_SEMS) * 2 + sems(6)[:1]
-    outs = [((rows, hidden), True)] * 2 + [(w1.shape, False), (w2.shape, False)]
-    kernel = functools.partial(mlp_kernel, layer, len(held))
-    return call(kernel, outs, scratch, 2 * layer, "mlp_block", 12 * total * hidden * cols, (y1, dy2, y2, dy1, w1, w2), held)
-
-
-def attn_block(layer, scale, x2, dy1, y1, dy2, wqkv, wo, held):
+    scratch += scatter_scratch(rows, hidden) * 2 + sems(AG_SEMS) * 2 + sems(RS_SEMS) * 2 + sems(11)[:1]
+    outs = [((rows, hidden), False, f32)] * 2 + [(w1.shape, False, f32), (w2.shape, False, f32), ((rows, hidden), False, bf16)]
+    kernel = functools.partial(mlp_kernel, layer, u is None, len(held))
+    given = () if u is None else (u,)
+    return call(kernel, outs, scratch, 2 * layer, "mlp_block", 12 * total * hidden * cols, 67043328, (y1, dy2, y2, dy1, w1, w2, *given), held)
+
+
+def attn_block(layer, scale, u, x2, dy1, y1, dy2, wqkv, wo, held):
     rows, hidden = x2.shape
     _, heads, _, head, _ = wqkv.shape
     width = heads * head
     total = 8 * rows
-    scratch = [vmem((rows, hidden), f32), vmem((heads, 3, head, hidden), f32), vmem((width, hidden), f32)] + [vmem((width, hidden), bf16)] * 3 + [vmem((8 * width, hidden), bf16)] + [vmem((total, hidden), bf16)] * 2
+    scratch = [vmem((rows, hidden), f32)] * 2 + [vmem((rows, hidden), bf16)]
+    scratch += [vmem((rows, hidden), f32), vmem((heads, 3, head, hidden), f32), vmem((width, hidden), f32)] + [vmem((width, hidden), bf16)] * 3 + [vmem((8 * width, hidden), bf16)] + [vmem((total, hidden), bf16)] * 2
     scratch += [vmem((total, width), bf16)] * 5 + [vmem((8, rows * width // 128, 128), bf16)] * 2
     scratch += [vmem((8, rows, width), bf16), vmem((4, rows * width // 256, 128), bf16), vmem((16, 256, 256), f32)]
-    scratch += scatter_scratch(rows // 2, hidden) * 2 + sems(AG_SEMS) * 3 + sems(13) + sems(RS_SEMS) * 2 + sems(11)[:1]
-    outs = [((rows, hidden), True)] * 2 + [(wqkv.shape, False), (wo.shape, False)]
-    kernel = functools.partial(attn_kernel, layer, scale, len(held))
-    return call(kernel, outs, scratch, 2 * layer + 1, "attn_block", 24 * total * hidden * width, (x2, dy1, y1, dy2, wqkv, wo), held)
+    scratch += scatter_scratch(rows // 2, hidden) * 2 + sems(AG_SEMS) * 3 + sems(13) + sems(RS_SEMS) * 2 + sems(20)[:1]
+    outs = [((rows, hidden), False, f32)] * 2 + [(wqkv.shape, False, f32), (wo.shape, False, f32)]
+    outs += [] if layer == 0 else [((rows, hidden), False, bf16)]
+    kernel = functools.partial(attn_kernel, layer, scale, layer == 0, len(held))
+    return call(kernel, outs, scratch, 2 * layer + 1, "attn_block", 24 * total * hidden * width, 67043328, (x2, dy1, y1, dy2, wqkv, wo, u), held)
 
 
 def local_backward(y_one, y_two, dy_one, dy_two, w_qkv, w_out, w_up, w_down):
@@ -601,12 +640,14 @@
     y_one, y_two, dy_one, dy_two = [x.reshape(-1, hidden) for x in (y_one, y_two, dy_one, dy_two)]
     w_qkv = w_qkv.transpose(0, 2, 3, 4, 1)
     w_out = w_out.reshape(n_layers, heads * head_dim, hidden)
-    held_mlp, held_attn = (), ()
+    held_mlp, held_attn, u_next = (), (), (None,)
     for layer in reversed(range(n_layers)):
-        y_two, dy_one, *held_mlp = mlp_block(layer, y_one, dy_two, y_two, dy_one, w_up, w_down, tuple(held_mlp))
-        y_one, dy_two, *held_attn = attn_block(
-            layer, head_dim ** -0.5, y_two, dy_one, y_one, dy_two, w_qkv, w_out, tuple(held_attn))
-    d_qkv, d_out, d_up, d_down = *held_attn, *held_mlp
+        y_two, dy_one, d_up, d_down, u_att = mlp_block(
+            layer, *u_next, y_one, dy_two, y_two, dy_one, w_up, w_down, held_mlp)
+        held_mlp = (d_up, d_down)
+        y_one, dy_two, d_qkv, d_out, *u_next = attn_block(
+            layer, head_dim ** -0.5, u_att, y_two, dy_one, y_one, dy_two, w_qkv, w_out, held_attn)
+        held_attn = (d_qkv, d_out)
     state = [x.reshape(state_shape) for x in (y_one, y_two, dy_one, dy_two)]
     return (*state, d_qkv.transpose(0, 4, 1, 2, 3), d_out.reshape(n_layers, heads, head_dim, hidden), d_up, d_down)
 

time: 514 us -> 510 us (level)
  no operation moved by 1% of the time
where the time goes in v4:
time: 510 us
  Pallas kernels  490 us (96%)
  local copies, waits for them, and re-layouts  19.6 us (4%)
    pallas_call x4, Pallas kernels, call(): pl.pallas_call(kernel, out_shape=[jax.ShapeDtypeStruct(shape, dtype) for...  490 us
    unnamed x26, local copies, waits for them, and re-layouts  19.6 us

profile of v4, /device:TPU:81, one launch (start us, length us, event | category | flops | bytes accessed | tf_op | source)
XLA Modules:
  0.0 509.9 jit_solution(16238231346885836351)
XLA Ops:
  0.6 135.0 %mlp_block.2 = (f32[256,1280]{1,0:T(8,128)}, f32[256,1280]{1,0:T(8,128)}, f32[2,1280,640]{2,1,0:T(8,128)}, f32[2,640,1280]{2,1,0:T(8,128)}, bf16[256,1280]{1,0:T(8,128)(2,1)}) custom-call(f32[256,1280]{1,0:T(8,128)} %bitcast.26, f32[256,1280]{1,0:T(8,128)} %bitcast.28, f32[256,1280]{1,0:T(8,128)} %bitcast.24, f32[256,1280]{1,0:T(8,128)} %bitcast.25, ...), custom_call_target="tpu_custom_call" | custom-call | flops 20132659200 | bytes 10000000 | tf_op jit(solution)/shard_map/mlp_block/pallas_call | solution.py:592
  135.7 111.4 %attn_block.2 = (f32[256,1280]{1,0:T(8,128)}, f32[256,1280]{1,0:T(8,128)}, f32[2,2,3,80,1280]{4,3,2,1,0:T(8,128)}, f32[2,160,1280]{2,1,0:T(8,128)}, bf16[256,1280]{1,0:T(8,128)(2,1)}) custom-call(f32[256,1280]{1,0:T(8,128)} %get-tuple-element.27.refs_0_.refs_2_, f32[256,1280]{1,0:T(8,128)} %get-tuple-element.28.refs_1_.refs_3_, f32[256,1280]{1,0:T(8,128)} %bitcast.27, ...), custom_call_target="tpu_custom_call" | custom-call | flops 10066329600 | bytes 10000000 | tf_op jit(solution)/shard_map/attn_block/pallas_call | solution.py:592
  247.1 132.3 %mlp_block.3 = (f32[256,1280]{1,0:T(8,128)}, f32[256,1280]{1,0:T(8,128)}, f32[2,1280,640]{2,1,0:T(8,128)}, f32[2,640,1280]{2,1,0:T(8,128)}, bf16[256,1280]{1,0:T(8,128)(2,1)}) custom-call(f32[256,1280]{1,0:T(8,128)} %get-tuple-element.30.refs_0_.refs_2_, ...), custom_call_target="tpu_custom_call", output_to_operand_aliasing={{2}: (7, {}), {3}: (8, {})} | custom-call | flops 20132659200 | bytes 10000000 | tf_op jit(solution)/shard_map/mlp_block/pallas_call | solution.py:592
  379.3 110.9 %attn_block.3 = (f32[256,1280]{1,0:T(8,128)}, f32[256,1280]{1,0:T(8,128)}, f32[2,2,3,80,1280]{4,3,2,1,0:T(8,128)}, f32[2,160,1280]{2,1,0:T(8,128)}) custom-call(f32[256,1280]{1,0:T(8,128)} %get-tuple-element.35.refs_0_, f32[256,1280]{1,0:T(8,128)} %get-tuple-element.36.refs_1_, ...), custom_call_target="tpu_custom_call", output_to_operand_aliasing={{2}: (7, {}), {3}: (8, {})} | custom-call | flops 10066329600 | bytes 10000000 | tf_op jit(solution)/shard_map/attn_block/pallas_call | solution.py:592
  490.3 0.0 copy-start.3
  490.3 2.6 copy.32
  492.9 0.0 copy-done.3
  492.9 0.0 copy-start.2
  492.9 0.0 copy-start.4
  492.9 1.1 copy.33
  493.9 0.7 copy-done.2
  494.7 1.1 copy.34
  495.7 0.0 copy-done.4
  495.7 1.1 copy.35
  496.8 1.3 copy-done
  498.1 2.5 copy.36
  500.6 0.5 copy-done.1
  501.1 1.2 copy.37
  502.3 0.0 slice-done
  502.3 0.1 slice-done.1
  502.4 3.3 copy.38
  505.7 0.0 slice-done.2
  505.7 1.4 slice-done.3
  507.1 2.8 copy.39
  (8 shorter events, 0.0 us)
Async XLA Ops:
  490.3 2.6 copy-start.3
  492.9 1.8 copy-start.2
  492.9 2.8 copy-start.4
  494.7 3.4 copy-start
  495.7 6.6 %slice-start = ((s8[6553600]{0:T(1024)(128)(4,1)}), s8[4194304]{0:T(1024)(128)(4,1)S(1)}, s32[]{:S(2)}) async-start(s8[6553600]{0:T(1024)(128)(4,1)} %bitcast.12), calls=%async_computation | async-start | bytes 8388608
  498.1 3.0 copy-start.1
  498.1 4.3 slice-start.1
  501.1 4.6 slice-start.2
  502.4 4.7 slice-start.3
